TPU v7x, 32 devices: a whole 2x2x4 slice. The times are simulated.
32 devices in a mesh: dp: 16 (over z, x, core), rep: 2 (over y).
Axes of the slice: x: 2, y: 2, z: 4, core: 2. Of those that a mesh axis runs over, the one named last changes fastest.
Arguments:
- tokens: bfloat16 [48, 261, 768], P('dp'), may hold values from -6 to 6
- text_len: int32 [48], P('dp'), may hold values from 1 to 64, as said below
- routes: int32 [48, 261], P('dp'), may hold values from 0 to 2, as said below
- attn_gain: float32 [768], replicated, may hold values from 0.5 to 1.5
- attn_shift: float32 [768], replicated, may hold values from -1 to 1
- w_qkv: bfloat16 [3, 768, 768], P(None, 'dp', 'rep'), may hold values from -0.21875 to 0.21875
- b_qv: float32 [2, 768], P(None, 'rep'), may hold values from -1.5 to 1.5
- w_out: bfloat16 [768, 768], P('dp', 'rep'), may hold values from -1.25 to 1.25
- b_out: float32 [768], replicated, may hold values from -0.5 to 0.5
- ffn_gain: float32 [768], replicated, may hold values from 0.5 to 1.5
- ffn_shift: float32 [768], replicated, may hold values from -1 to 1
- w_up: bfloat16 [3, 768, 3072], P(None, 'dp', 'rep'), may hold values from -0.21875 to 0.21875
- b_up: float32 [3, 3072], P(None, 'rep'), may hold values from -1.5 to 1.5
- w_down: bfloat16 [3, 768, 3072], P(None, 'dp', 'rep'), may hold values from -0.15625 to 0.15625
- b_down: float32 [3, 768], replicated, may hold values from -0.5 to 0.5
- cotangent: bfloat16 [48, 261, 768], P('dp'), may hold values from -6 to 6
Outputs:
- output: bfloat16 [48, 261, 768], P('dp')
- grad_tokens: float32 [48, 261, 768], P('dp')
- grad_w_qkv: float32 [3, 768, 768], P(None, 'dp', 'rep')
- grad_w_out: float32 [768, 768], P('dp', 'rep')
- grad_w_up: float32 [3, 768, 3072], P(None, 'dp', 'rep')
- grad_w_down: float32 [3, 768, 3072], P(None, 'dp', 'rep')
- grad_b_qv: float32 [2, 768], P(None, 'rep')
- grad_b_out: float32 [768], replicated
- grad_b_up: float32 [3, 3072], P(None, 'rep')
- grad_b_down: float32 [3, 768], replicated
- grad_norms: float32 [4, 768], replicated
Inputs may be any that keep to these rules, and one draw needn't show every extreme that they name: `text_len`: text rows in use of each item; some item uses all 64 in every draw. `routes`: routing by modality: each item either sends its first 197 rows to expert 0 and its other rows to expert 1, or sends all its rows to expert 2; both kinds of item occur in every draw.
All inputs are finite; a program needn't handle non-finite values.
Results may differ from a plain program's by a relative error of at most 0.014.
Values may be sent and summed in bfloat16 or wider, within the bound.
No kernel may reach another device: no remote copies, remote signals or barrier semaphores. Data moves between devices by JAX's collectives and lax.ppermute only.
A program may use at most 192 MiB of HBM per device.

v0:
```python
import math

import jax
import jax.numpy as jnp
from jax import lax
from jax.sharding import PartitionSpec as P

HDIM = 64
IMG = 197


EPSILON = 1e-05
TILE = 128
ROOT_HALF = 0.7071067811865476
INV_ROOT_TAU = 0.3989422804014327
HIGHEST = lax.Precision.HIGHEST


def norm_rows(vector, gain_vec, shift_vec):
    row_mean = jnp.mean(vector, axis=-1, keepdims=True)
    centred = vector - row_mean
    row_var = jnp.mean(centred * centred, axis=-1, keepdims=True)
    spread = lax.rsqrt(row_var + EPSILON)
    normal_rows = centred * spread
    return (normal_rows * gain_vec + shift_vec, normal_rows, spread)


def norm_back(grad_rows, normal_rows, spread, gain_vec):
    scaled = grad_rows * gain_vec
    return spread * (
        scaled
        - jnp.mean(scaled, axis=-1, keepdims=True)
        - normal_rows * jnp.mean(scaled * normal_rows, axis=-1, keepdims=True)
    )


def gelu_slope(pre_act):
    return (
        0.5 * (1.0 + lax.erf(pre_act * ROOT_HALF))
        + pre_act * jnp.exp(-0.5 * pre_act * pre_act) * INV_ROOT_TAU
    )


def packing(route_flat, expert_count, row_count):
    tile_count = -(-row_count // TILE) + expert_count
    route_hits = (route_flat[:, None] == jnp.arange(expert_count, dtype=jnp.int32)[None, :]).astype(
        jnp.int32
    )
    counts = jnp.sum(route_hits, axis=0)
    padded = (counts + TILE - 1) // TILE * TILE
    group_end = jnp.cumsum(padded)
    group_start = group_end - padded
    before = jnp.cumsum(route_hits, axis=0) - route_hits
    target = jnp.sum(route_hits * (before + group_start[None, :]), axis=1)
    tile_start = jnp.arange(tile_count, dtype=jnp.int32) * TILE
    tile_owner = jnp.minimum(
        jnp.sum((tile_start[:, None] >= group_end[None, :]).astype(jnp.int32), axis=1),
        expert_count - 1,
    )
    return (target, tile_owner, tile_count)


def per_device(
    tokens,
    text_len,
    routes,
    attn_gain,
    attn_shift,
    w_qkv,
    b_qv,
    w_out,
    b_out,
    ffn_gain,
    ffn_shift,
    w_up,
    b_up,
    w_down,
    b_down,
    cotangent,
):
    item_count, seq_len, model_width = tokens.shape
    row_count = item_count * seq_len
    local_width = w_qkv.shape[2]
    local_heads = local_width // HDIM
    expert_count = w_up.shape[0]
    score_scale = 1.0 / math.sqrt(HDIM)
    contract_last = (((1,), (1,)), ((), ()))
    contract_first = (((0,), (0,)), ((), ()))
    inputs = tokens.reshape(row_count, model_width).astype(jnp.float32)
    first_normed, first_hat, first_spread = norm_rows(inputs, attn_gain, attn_shift)
    first_low = first_normed.astype(jnp.bfloat16)
    qkv_full, out_full = (
        lax.all_gather(w_qkv, "dp", axis=1, tiled=True),
        lax.all_gather(w_out, "dp", axis=0, tiled=True),
    )
    projected = jnp.einsum("rd,tde->tre", first_low, qkv_full, preferred_element_type=jnp.float32)
    bias_rows = jnp.stack([b_qv[0], jnp.zeros_like(b_qv[0]), b_qv[1]])
    proj_low = (projected + bias_rows[:, None, :]).astype(jnp.bfloat16)
    head_split = proj_low.reshape(3, item_count, seq_len, local_heads, HDIM)
    queries, key_rows, values = (head_split[0], head_split[1], head_split[2])
    key_ok = jnp.arange(seq_len, dtype=jnp.int32)[None, :] < (IMG + text_len)[:, None]

    def scores_of(query_part, key_part):
        raw_scores = (
            jnp.einsum("ishd,ijhd->ihsj", query_part, key_part, preferred_element_type=jnp.float32)
            * score_scale
        )
        return jnp.where(key_ok[:, None, None, :], raw_scores, -1e30)

    raw_scores = scores_of(queries, key_rows)
    row_max = jnp.max(raw_scores, axis=-1, keepdims=True)
    raised = jnp.exp(raw_scores - row_max)
    row_total = jnp.sum(raised, axis=-1, keepdims=True)
    attn_probs = raised / row_total
    log_total = row_max + jnp.log(row_total)
    probs_low = attn_probs.astype(jnp.bfloat16)
    context = jnp.einsum("ihsj,ijhd->ishd", probs_low, values, preferred_element_type=jnp.float32)
    context_low = context.reshape(row_count, local_width).astype(jnp.bfloat16)
    attn_part = lax.dot_general(
        context_low, out_full, contract_last, preferred_element_type=jnp.float32
    )
    attn_share = lax.psum_scatter(
        attn_part.astype(jnp.bfloat16), "rep", scatter_dimension=1, tiled=True
    ).astype(jnp.float32)
    attn_sum = lax.all_gather(attn_share.astype(jnp.bfloat16), "rep", axis=1, tiled=True).astype(
        attn_share.dtype
    )
    residual = inputs + (attn_sum + b_out)
    second_normed, second_hat, second_spread = norm_rows(residual, ffn_gain, ffn_shift)
    second_low = second_normed.astype(jnp.bfloat16)
    route_flat = routes.reshape(row_count)
    target, tile_owner, tile_count = packing(route_flat, expert_count, row_count)
    packed_input = (
        jnp.zeros((tile_count * TILE, model_width), jnp.bfloat16)
        .at[target]
        .set(second_low)
        .reshape(tile_count, TILE, model_width)
    )
    up_full, down_full = (
        lax.all_gather(w_up, "dp", axis=1, tiled=True),
        lax.all_gather(w_down, "dp", axis=1, tiled=True),
    )
    owner_hot = (tile_owner[:, None] == jnp.arange(expert_count, dtype=jnp.int32)[None, :]).astype(
        jnp.float32
    )
    up_projection_tiles = up_full[tile_owner]
    down_projection_tiles = down_full[tile_owner]
    pre_acts = (
        jnp.einsum(
            "pim,pmj->pij", packed_input, up_projection_tiles, preferred_element_type=jnp.float32
        )
        + jnp.dot(owner_hot, b_up, precision=HIGHEST)[:, None, :]
    )
    activated_rows = jax.nn.gelu(pre_acts, approximate=False).astype(jnp.bfloat16)
    partial_sums = jnp.einsum(
        "wmy,wny->wmn", activated_rows, down_projection_tiles, preferred_element_type=jnp.float32
    )
    ffn_rows = partial_sums.reshape(tile_count * TILE, model_width)[target]
    ffn_share = lax.psum_scatter(
        ffn_rows.astype(jnp.bfloat16), "rep", scatter_dimension=1, tiled=True
    ).astype(jnp.float32)
    ffn_sum = lax.all_gather(ffn_share.astype(jnp.bfloat16), "rep", axis=1, tiled=True).astype(
        ffn_share.dtype
    )
    route_pick = (route_flat[:, None] == jnp.arange(expert_count, dtype=jnp.int32)[None, :]).astype(
        jnp.float32
    )
    output = residual + (ffn_sum + jnp.dot(route_pick, b_down, precision=HIGHEST))
    output_low = output.astype(jnp.bfloat16).reshape(item_count, seq_len, model_width)
    grad_low = cotangent.reshape(row_count, model_width)
    grad_out = grad_low.astype(jnp.float32)
    grad_b_down = jnp.dot(route_pick.T, grad_out, precision=HIGHEST)
    up_back, down_back, qkv_back, out_back = (
        lax.all_gather(w_up, "dp", axis=1, tiled=True),
        lax.all_gather(w_down, "dp", axis=1, tiled=True),
        lax.all_gather(w_qkv, "dp", axis=1, tiled=True),
        lax.all_gather(w_out, "dp", axis=0, tiled=True),
    )
    up_gradient_tiles = up_back[tile_owner]
    down_gradient_tiles = down_back[tile_owner]
    packed_gradient = (
        jnp.zeros((tile_count * TILE, model_width), jnp.bfloat16)
        .at[target]
        .set(grad_low)
        .reshape(tile_count, TILE, model_width)
    )
    grad_active = jnp.einsum(
        "pim,pmj->pij", packed_gradient, down_gradient_tiles, preferred_element_type=jnp.float32
    )
    gradient_before_activation = (grad_active * gelu_slope(pre_acts)).astype(jnp.bfloat16)
    grad_tiles = jnp.einsum(
        "wmy,wny->wmn",
        gradient_before_activation,
        up_gradient_tiles,
        preferred_element_type=jnp.float32,
    )
    down_terms = jnp.einsum(
        "jxa,jxm->jam", packed_gradient, activated_rows, preferred_element_type=jnp.float32
    )
    grad_down_local = jnp.einsum("te,tdf->edf", owner_hot, down_terms, precision=HIGHEST)
    up_projection_terms = jnp.einsum(
        "jxa,jxm->jam", packed_input, gradient_before_activation, preferred_element_type=jnp.float32
    )
    grad_up_local = jnp.einsum("te,tdf->edf", owner_hot, up_projection_terms, precision=HIGHEST)
    grad_b_up = jnp.dot(
        owner_hot.T,
        jnp.sum(gradient_before_activation.astype(jnp.float32), axis=1),
        precision=HIGHEST,
    )
    back_rows = grad_tiles.reshape(tile_count * TILE, model_width)[target]
    second_share = lax.psum_scatter(
        back_rows.astype(jnp.bfloat16), "rep", scatter_dimension=1, tiled=True
    ).astype(jnp.float32)
    grad_second = lax.all_gather(
        second_share.astype(jnp.bfloat16), "rep", axis=1, tiled=True
    ).astype(second_share.dtype)
    grad_ffn_gain = jnp.sum(grad_second * second_hat, axis=0)
    grad_ffn_shift = jnp.sum(grad_second, axis=0)
    grad_residual = grad_out + norm_back(grad_second, second_hat, second_spread, ffn_gain)
    grad_w_up, grad_w_down = (
        lax.psum_scatter(grad_up_local, "dp", scatter_dimension=1, tiled=True),
        lax.psum_scatter(grad_down_local, "dp", scatter_dimension=1, tiled=True),
    )
    grad_branch = grad_residual.astype(jnp.bfloat16)
    grad_b_out = jnp.sum(grad_branch.astype(jnp.float32), axis=0)
    grad_context = jnp.dot(grad_branch, out_back, preferred_element_type=jnp.float32)
    grad_ctx_low = grad_context.astype(jnp.bfloat16).reshape(item_count, seq_len, local_heads, HDIM)
    grad_out_local = lax.dot_general(
        grad_branch, context_low, contract_first, preferred_element_type=jnp.float32
    )
    again_scores = scores_of(queries, key_rows)
    again_probs = jnp.exp(again_scores - log_total)
    again_low = again_probs.astype(jnp.bfloat16)
    grad_probs = jnp.einsum(
        "ishd,ijhd->ihsj", grad_ctx_low, values, preferred_element_type=jnp.float32
    )
    grad_values = jnp.einsum(
        "ihsj,ishd->ijhd", again_low, grad_ctx_low, preferred_element_type=jnp.float32
    )
    inner_sum = jnp.sum(again_probs * grad_probs, axis=-1, keepdims=True)
    grad_scores = (again_probs * (grad_probs - inner_sum)).astype(jnp.bfloat16)
    grad_queries = (
        jnp.einsum("ihsj,ijhd->ishd", grad_scores, key_rows, preferred_element_type=jnp.float32)
        * score_scale
    )
    grad_keys = (
        jnp.einsum("ihsj,ishd->ijhd", grad_scores, queries, preferred_element_type=jnp.float32)
        * score_scale
    )
    grad_proj = (
        jnp.stack([grad_queries, grad_keys, grad_values])
        .reshape(3, row_count, local_width)
        .astype(jnp.bfloat16)
    )
    grad_b_qv = jnp.stack(
        [
            jnp.sum(grad_proj[0].astype(jnp.float32), axis=0),
            jnp.sum(grad_proj[2].astype(jnp.float32), axis=0),
        ]
    )
    grad_qkv_local = jnp.einsum(
        "rd,tre->tde", first_low, grad_proj, preferred_element_type=jnp.float32
    )
    back_first = jnp.einsum("tre,tde->rd", grad_proj, qkv_back, preferred_element_type=jnp.float32)
    first_share = lax.psum_scatter(
        back_first.astype(jnp.bfloat16), "rep", scatter_dimension=1, tiled=True
    ).astype(jnp.float32)
    grad_first = lax.all_gather(first_share.astype(jnp.bfloat16), "rep", axis=1, tiled=True).astype(
        first_share.dtype
    )
    grad_attn_gain = jnp.sum(grad_first * first_hat, axis=0)
    grad_attn_shift = jnp.sum(grad_first, axis=0)
    grad_inputs = grad_residual + norm_back(grad_first, first_hat, first_spread, attn_gain)
    grad_w_qkv, grad_w_out = (
        lax.psum_scatter(grad_qkv_local, "dp", scatter_dimension=1, tiled=True),
        lax.psum_scatter(grad_out_local, "dp", scatter_dimension=0, tiled=True),
    )
    norm_local = jnp.stack([grad_attn_gain, grad_attn_shift, grad_ffn_gain, grad_ffn_shift])
    total_qv, total_out, total_up, total_down, total_norms = lax.psum(
        (grad_b_qv, grad_b_out, grad_b_up, grad_b_down, norm_local), "dp"
    )
    return (
        output_low,
        grad_inputs.reshape(item_count, seq_len, model_width),
        grad_w_qkv,
        grad_w_out,
        grad_w_up,
        grad_w_down,
        total_qv,
        total_out,
        total_up,
        total_down,
        total_norms,
    )


def solution(mesh):
    return jax.shard_map(
        per_device,
        mesh=mesh,
        in_specs=(
            P("dp", None, None),
            P("dp"),
            P("dp", None),
            P(),
            P(),
            P(None, "dp", "rep"),
            P(None, "rep"),
            P("dp", "rep"),
            P(),
            P(),
            P(),
            P(None, "dp", "rep"),
            P(None, "rep"),
            P(None, "dp", "rep"),
            P(),
            P("dp", None, None),
        ),
        out_specs=(
            P("dp", None, None),
            P("dp", None, None),
            P(None, "dp", "rep"),
            P("dp", "rep"),
            P(None, "dp", "rep"),
            P(None, "dp", "rep"),
            P(None, "rep"),
            P(),
            P(None, "rep"),
            P(),
            P(),
        ),
        check_vma=False,
    )
```

profile of v0, /device:TPU:0, one launch (start us, length us, event | category | flops | bytes accessed | tf_op | source)
XLA Modules:
  0.0 1421.5 jit_solution(17374396237260171322)
XLA Ops:
  14.2 27.1 %all_gather.29 = bf16[768,384]{1,0:T(8,128)(2,1)} all-gather(bf16[48,384]{1,0:T(8,128)(2,1)S(1)} %copy-done.33), channel_id=1, replica_groups=mesh['dp'=16,'rep'=2] {'dp'}, dimensions={0}, use_global_device_ids=true | all-gather | bytes 626688 | tf_op jit(solution)/shard_map/all_gather | solution.py:94
  41.3 13.2 all-gather.8.cloned.1.call-done
  79.3 22.8 %reduce-scatter.16.cloned.1.call-done = bf16[384,783]{1,0:T(8,128)(2,1)} async-done(((bf16[768,783]{1,0:T(8,128)(2,1)}), bf16[384,783]{1,0:T(8,128)(2,1)}) %reduce-scatter.16.cloned.1.call-update) | async-done | bytes 601360
  117.0 10.5 all-gather.10.cloned.1.call-done
  130.4 7.9 scatter_custom_fusion
  138.3 57.5 %all-gather.12.cloned.1.call-done = bf16[3,768,1536]{2,1,0:T(8,128)(2,1)} async-done(((bf16[3,48,1536]{2,1,0:T(8,128)(2,1)}), bf16[3,768,1536]{2,1,0:T(8,128)(2,1)}) %all-gather.12.cloned.1.call-update) | async-done | bytes 7077904 | tf_op jit(solution)/shard_map/all_gather | solution.py:140
  202.2 8.0 gather_fusion.2
  210.2 7.8 gather_fusion.3
  218.0 10.1 constant_dynamic-update-slice_fusion.1
  228.1 34.7 %all-gather.14.cloned.1.call-done = bf16[3,768,1536]{2,1,0:T(8,128)(2,1)} async-done(((bf16[3,48,1536]{2,1,0:T(8,128)(2,1)}), bf16[3,768,1536]{2,1,0:T(8,128)(2,1)}) %all-gather.14.cloned.1.call-update) | async-done | bytes 7077904 | tf_op jit(solution)/shard_map/all_gather | solution.py:141
  276.9 10.1 constant_dynamic-update-slice_fusion.3
  294.8 10.6 constant_dynamic-update-slice_fusion
  312.1 14.1 fusion.22
  326.2 15.7 %convert_reduce_fusion = (f32[10,1536]{1,0:T(8,128)}, bf16[10,128,1536]{2,1,0:T(8,128)(2,1)}) fusion(f32[10,128,1536]{2,1,0:T(8,128)} %get-tuple-element.99, f32[10,1536]{1,0:T(8,128)S(1)} %fusion.73, bf16[10,128,768]{2,1,0:T(8,128)(2,1)S(1)} %bitcast.105, bf16[10,768,1536]{2,1,0:T(8,128)(2,1)} %constant_dynamic-update-slice_fusion.2), kind=kOutput, calls=%fused_computation.28 | convolution fusion | flops 3045442560 | bytes 37478400 | tf_op jit(solution)/shard_map/pim,pmj->pij/dot_general | solution.py:187
  341.9 14.0 fusion.100
  365.0 20.1 %fusion.6 = bf16[10,128,1536]{2,1,0:T(8,128)(2,1)} fusion(f32[10,128,1536]{2,1,0:T(8,128)} %get-tuple-element.99, f32[10,1536]{1,0:T(8,128)S(1)} %fusion.73, u16[128,1536]{1,0:T(8,128)(2,1)} %get-tuple-element.67, u16[128,1536]{1,0:T(8,128)(2,1)} %get-tuple-element.66), kind=kLoop, calls=%fused_computation.16 | loop fusion | flops 139591680 | bytes 12644352 | tf_op jit(solution)/shard_map/convert_element_type | solution.py:154
  385.1 13.7 fusion.99
  410.1 20.8 %fusion.101 = f32[10,768,1536]{2,1,0:T(8,128)} fusion(bf16[10,128,768]{2,1,0:T(8,128)(2,1)} %bitcast.103, bf16[10,128,1536]{2,1,0:T(8,128)(2,1)} %get-tuple-element.103), kind=kOutput, calls=%fused_computation.193 | convolution fusion | flops 3019898880 | bytes 53084160 | tf_op jit(solution)/shard_map/jxa,jxm->jam/dot_general | solution.py:201
  476.3 67.2 %fusion.2 = f32[3,768,1536]{2,0,1:T(4,128)} fusion(f32[10,768,1536]{2,1,0:T(8,128)} %fusion.101, s32[10]{0:T(128)S(1)} %copy-done.43), kind=kOutput, calls=%fused_computation.10 | convolution fusion | flops 424673312 | bytes 61341736 | tf_op jit(solution)/shard_map/te,tdf->edf/dot_general | solution.py:204
  545.8 21.0 %fusion.102 = f32[10,768,1536]{2,1,0:T(8,128)} fusion(bf16[10,128,768]{2,1,0:T(8,128)(2,1)S(1)} %bitcast.106, bf16[10,128,1536]{2,1,0:T(8,128)(2,1)} %fusion.6), kind=kOutput, calls=%fused_computation.194 | convolution fusion | flops 3019898880 | bytes 53084160 | tf_op jit(solution)/shard_map/jxa,jxm->jam/dot_general | solution.py:197
  569.1 67.0 %fusion = f32[3,768,1536]{2,0,1:T(4,128)} fusion(f32[10,768,1536]{2,1,0:T(8,128)} %fusion.102, s32[10]{0:T(128)S(1)} %copy-done.43), kind=kOutput, calls=%fused_computation.8 | convolution fusion | flops 424673312 | bytes 61341736 | tf_op jit(solution)/shard_map/te,tdf->edf/dot_general | solution.py:200
  671.7 65.4 %all-reduce.4 = (f32[2,384]{1,0:T(2,128)}, f32[768]{0:T(1024)}, f32[3,1536]{1,0:T(4,128)}, f32[3,768]{1,0:T(4,128)}, f32[4,768]{1,0:T(4,128)}) all-reduce(f32[2,384]{1,0:T(2,128)S(1)} %pad_maximum_fusion.5, f32[768]{0:T(1024)S(1)} %get-tuple-element.84, f32[3,1536]{1,0:T(4,128)S(1)} %fusion.71, ...), channel_id=1, replica_groups=mesh['dp'=16,'rep'=2] {'dp'}, use_global_device_ids=true, to_apply=%region_29.30 | all-reduce | flops 11520 | bytes 92160 | tf_op jit(solution)/shard_map/psum | solution.py:279
  737.0 615.4 %all-reduce.8.cloned.1.call-done = (f32[3,768,384]{2,0,1:T(4,128)}, f32[3,768,1536]{2,0,1:T(4,128)}, f32[3,768,1536]{2,0,1:T(4,128)}) async-done(((f32[3,768,384]{2,0,1:T(4,128)}, f32[3,768,1536]{2,0,1:T(4,128)}, f32[3,768,1536]{2,0,1:T(4,128)}), (f32[3,768,384]{2,0,1:T(4,128)}, f32[3,768,1536]{2,0,1:T(4,128)}, f32[3,768,1536]{2,0,1:T(4,128)})) %all-reduce.8.cloned.1.call-update) | async-done | bytes 31850512
  1359.4 55.4 %reduce-scatter.14.cloned.1.call-done = f32[48,384]{1,0:T(8,128)} async-done(((f32[768,384]{1,0:T(8,128)}), f32[48,384]{1,0:T(8,128)}) %reduce-scatter.14.cloned.1.call-update) | async-done | bytes 73744 | tf_op jit(solution)/shard_map/reduce_scatter | solution.py:276
  (260 shorter events, 196.1 us)
Async XLA Ops:
  7.2 109.5 %copy-start = (f32[3,1536]{1,0:T(4,128)S(1)}, f32[3,1536]{1,0:T(4,128)}, u32[]{:S(2)}) copy-start(f32[3,1536]{1,0:T(4,128)} %param.28) | copy-start | bytes 55300
  7.2 47.3 %copy-start.48 = (f32[768]{0:T(1024)S(1)}, f32[768]{0:T(1024)}, u32[]{:S(2)}) copy-start(f32[768]{0:T(1024)} %param.20) | copy-start | bytes 9220
  7.2 47.2 %all-gather.8.cloned.1.call-start = ((), (), s32[]{:S(2)}) async-start(), calls=%async_computation.5 | async-start | bytes 1880064 | tf_op jit(solution)/shard_map/all_gather | solution.py:93
  8.0 94.1 %reduce-scatter.16.cloned.1.call-start = ((), (), s32[]{:S(2)}) async-start(), calls=%async_computation.13 | async-start | bytes 2064384
  9.6 48.4 %copy-start.6 = (f32[783,768]{1,0:T(8,128)}, f32[783,768]{1,0:T(8,128)S(1)}, u32[]{:S(2)}) copy-start(f32[783,768]{1,0:T(8,128)S(1)} %reshape.320) | copy-start | bytes 7216132
  79.3 48.2 %all-gather.10.cloned.1.call-start = ((), (), s32[]{:S(2)}) async-start(), calls=%async_computation.6 | async-start | bytes 1806336 | tf_op jit(solution)/shard_map/all_gather | solution.py:125
  104.3 91.4 %all-gather.12.cloned.1.call-start = ((), (), s32[]{:S(2)}) async-start(), calls=%async_computation.7 | async-start | bytes 7520256 | tf_op jit(solution)/shard_map/all_gather | solution.py:140
  104.9 157.8 %all-gather.14.cloned.1.call-start = ((), (), s32[]{:S(2)}) async-start(), calls=%async_computation.8 | async-start | bytes 7520256 | tf_op jit(solution)/shard_map/all_gather | solution.py:141
  105.5 302.4 %reduce-scatter.20.cloned.1.call-start = ((), (), s32[]{:S(2)}) async-start(), calls=%async_computation.15 | async-start | bytes 2064384
  129.9 304.8 %copy-start.3 = (f32[783,768]{1,0:T(8,128)}, f32[783,768]{1,0:T(8,128)S(1)}, u32[]{:S(2)}) copy-start(f32[783,768]{1,0:T(8,128)S(1)} %get-tuple-element.87) | copy-start | bytes 7216132
  365.0 67.1 %all-gather.18.cloned.1.call-start = ((), (), s32[]{:S(2)}) async-start(), calls=%async_computation.10 | async-start | bytes 1806336 | tf_op jit(solution)/shard_map/all_gather | solution.py:214
  410.1 133.4 %reduce-scatter.18.cloned.1.call-start = ((), (), s32[]{:S(2)}) async-start(), calls=%async_computation.14 | async-start | bytes 2064384
  431.0 135.8 %reduce-scatter.22.cloned.1.call-start = ((), (), s32[]{:S(2)}) async-start(), calls=%async_computation.16 | async-start | bytes 2064384
  476.2 69.5 %copy-start.20 = (bf16[1280,768]{1,0:T(8,128)(2,1)S(1)}, bf16[1280,768]{1,0:T(8,128)(2,1)}, u32[]{:S(2)}) copy-start(bf16[1280,768]{1,0:T(8,128)(2,1)} %scatter_custom_fusion.1) | copy-start | bytes 5898244
  476.2 175.2 %all-gather.16.cloned.1.call-start = ((), (), s32[]{:S(2)}) async-start(), calls=%async_computation.9 | async-start | bytes 1806336 | tf_op jit(solution)/shard_map/all_gather | solution.py:162
  545.7 117.8 %all-gather.20.cloned.1.call-start = ((), (), s32[]{:S(2)}) async-start(), calls=%async_computation.11 | async-start | bytes 1806336 | tf_op jit(solution)/shard_map/all_gather | solution.py:268
  569.0 67.1 %copy-start.7 = (f32[783,768]{1,0:T(8,128)S(1)}, f32[783,768]{1,0:T(8,128)}, u32[]{:S(2)}) copy-start(f32[783,768]{1,0:T(8,128)} %copy-done.6) | copy-start | bytes 7216132
  569.0 67.1 %copy-start.36 = (f32[783]{0:T(1024)S(1)}, f32[783]{0:T(1024)}, u32[]{:S(2)}) copy-start(f32[783]{0:T(1024)} %copy-done.35) | copy-start | bytes 9400
  569.0 67.1 %copy-start.38 = (f32[783]{0:T(1024)S(1)}, f32[783]{0:T(1024)}, u32[]{:S(2)}) copy-start(f32[783]{0:T(1024)} %copy-done.37) | copy-start | bytes 9400
  569.0 67.1 %copy-start.40 = (f32[768]{0:T(1024)S(1)}, f32[768]{0:T(1024)}, u32[]{:S(2)}) copy-start(f32[768]{0:T(1024)} %param.19) | copy-start | bytes 9220
  569.0 67.1 %copy-start.49 = (f32[768]{0:T(1024)S(1)}, f32[768]{0:T(1024)}, u32[]{:S(2)}) copy-start(f32[768]{0:T(1024)} %param.20) | copy-start | bytes 9220
  569.0 783.3 %all-reduce.8.cloned.1.call-start = ((), (), s32[]{:S(2)}) async-start(), calls=%async_computation.17 | async-start | bytes 84934656
  647.8 767.0 %reduce-scatter.14.cloned.1.call-start = ((), (), s32[]{:S(2)}) async-start(), calls=%async_computation.12 | async-start | bytes 1253376 | tf_op jit(solution)/shard_map/reduce_scatter | solution.py:276
  1354.1 60.7 %copy-start.1 = (f32[3,1536]{1,0:T(4,128)S(1)}, f32[3,1536]{1,0:T(4,128)}, u32[]{:S(2)}) copy-start(f32[3,1536]{1,0:T(4,128)} %param.28) | copy-start | bytes 55300
  (43 other events, 413.2 us)
Sparse Core Ops, SparseCore 0:
  10.4 44.0 all-gather.7
  79.4 22.6 reduce-scatter.15
  104.4 23.0 all-gather.9
  129.6 66.0 all-gather.11
  197.9 64.8 all-gather.13
  365.1 22.7 reduce-scatter.19
  410.2 21.8 all-gather.17
  434.3 23.9 reduce-scatter.17
  476.3 24.3 reduce-scatter.21
  545.8 23.3 all-gather.15
  570.8 23.0 all-gather.19
  647.9 704.3 all-reduce.7
  1356.5 58.1 reduce-scatter.13
where the time goes:
time: 1430 us; the launch traced here: 1420 us
  waiting for transfers between devices  812 us (57%)
  matrix products  278 us (19%)
  local copies, waits for them, and re-layouts  170 us (12%)
  blocking collectives  92.4 us (6%)
  other arithmetic  52.1 us (4%)
  between operations  15.8 us (1%)
    unnamed x18, waiting for transfers between devices  640 us
    dot_general x1, matrix products, per_device(): jnp.einsum('te,tdf->edf', owner_hot, up_projection_terms, precision=HIGHEST)  67.2 us
    unnamed x128, local copies, waits for them, and re-layouts  67 us
    dot_general x1, matrix products, per_device(): jnp.einsum('te,tdf->edf', owner_hot, down_terms, precision=HIGHEST)  67 us
    psum x1, blocking collectives, per_device(): lax.psum((grad_b_qv, grad_b_out, grad_b_up, grad_b_down, norm_local), 'dp')  65.4 us
    all_gather x1, waiting for transfers between devices, per_device(): lax.all_gather(w_up, 'dp', axis=1, tiled=True)  57.5 us
    reduce_scatter x1, waiting for transfers between devices, per_device(): lax.psum_scatter(grad_out_local, 'dp', scatter_dimension=0, tiled=True)  55.4 us
    all_gather x1, waiting for transfers between devices, per_device(): lax.all_gather(w_down, 'dp', axis=1, tiled=True)  34.7 us
  transfers between devices with their start and end apart: 13, of which 8 were waited for; matrix products, arithmetic and copies ran while one was open for 26% of the time, Pallas kernels for 0%

commit v1 on v0

v1 whole, which is shorter than its diff:
```python
import functools
import math

import jax
import jax.numpy as jnp
from jax import lax
from jax.experimental import pallas as pl
from jax.experimental.pallas import tpu as pltpu
from jax.sharding import PartitionSpec as P

HDIM = 64
IMG = 197
EPSILON = 1e-05
ROOT_HALF = 0.7071067811865476
INV_ROOT_TAU = 0.3989422804014327
SUB = 16
LANES = 128
BF = jnp.bfloat16
F32 = jnp.float32

NN = (((1,), (0,)), ((), ()))
NT = (((1,), (1,)), ((), ()))
TN = (((0,), (0,)), ((), ()))


def up_to(n, m):
    return -(-n // m) * m


def dot(a, b, dims):
    return lax.dot_general(a, b, dims, preferred_element_type=F32)


def full(shape):
    zeros = (0,) * len(shape)
    return pl.BlockSpec(shape, lambda *_: zeros)


def per_item(shape):
    zeros = (0,) * (len(shape) - 1)
    return pl.BlockSpec(shape, lambda i, *_: (i,) + zeros)


ANY = pl.BlockSpec(memory_space=pl.ANY)


def params():
    return pltpu.CompilerParams(vmem_limit_bytes=60 * 1024 * 1024)


def cost(flops, nbytes, trans=0):
    return pl.CostEstimate(flops=int(flops), transcendentals=int(trans), bytes_accessed=int(nbytes))


def normed(v):
    centred = v - jnp.mean(v, axis=-1, keepdims=True)
    var = jnp.mean(centred * centred, axis=-1, keepdims=True)
    spread = lax.rsqrt(var + EPSILON)
    return centred * spread, spread


def norm_back(grad, hat, spread, gain):
    scaled = grad * gain
    return spread * (
        scaled
        - jnp.mean(scaled, axis=-1, keepdims=True)
        - hat * jnp.mean(scaled * hat, axis=-1, keepdims=True)
    )


def place_copies(off_ref, pieces, dest, sems):
    copies = []
    for n, piece in enumerate(pieces):
        subs, _, rows, _ = piece.shape
        for j in range(subs):
            at = off_ref[n * subs + j]
            copies.append(
                pltpu.make_async_copy(
                    piece.at[j],
                    dest.at[:, pl.ds(pl.multiple_of(at, SUB), rows), :],
                    sems.at[n * subs + j],
                )
            )
    return copies


def k_proj(off_ref, tok_ref, gain_ref, shift_ref, bias_ref, *rest):
    a_ref, qkv_ref, w_ref, sems = rest[-4:]
    pieces = rest[:-4]
    first = pl.program_id(0) == 0

    @pl.when(first)
    def _():
        for c in place_copies(off_ref, pieces, w_ref, sems):
            c.start()

    hat, _ = normed(tok_ref[0].astype(F32))
    a_ref[0] = (hat * gain_ref[...] + shift_ref[...]).astype(BF)

    @pl.when(first)
    def _():
        for c in place_copies(off_ref, pieces, w_ref, sems):
            c.wait()

    a = a_ref[0]
    for t in range(3):
        qkv_ref[t, 0] = (dot(a, w_ref[t], NN) + bias_ref[t : t + 1, :]).astype(BF)


def project(tokens, gain, shift, bias, pieces, offsets):
    items, rows, width = tokens.shape
    planes, cols = pieces[0].shape[1], pieces[0].shape[3]
    count = len(pieces) * pieces[0].shape[0]
    grid_spec = pltpu.PrefetchScalarGridSpec(
        num_scalar_prefetch=1,
        grid=(items,),
        in_specs=[
            per_item((1, rows, width)),
            full((1, width)),
            full((1, width)),
            full((3, cols)),
        ]
        + [ANY] * len(pieces),
        out_specs=[
            per_item((1, rows, width)),
            pl.BlockSpec((3, 1, rows, cols), lambda i, *_: (0, i, 0, 0)),
            full((planes, width, cols)),
        ],
        scratch_shapes=[pltpu.SemaphoreType.DMA((count,))],
    )
    return pl.pallas_call(
        k_proj,
        grid_spec=grid_spec,
        out_shape=[
            jax.ShapeDtypeStruct((items, rows, width), BF),
            jax.ShapeDtypeStruct((3, items, rows, cols), BF),
            jax.ShapeDtypeStruct((planes, width, cols), BF),
        ],
        compiler_params=params(),
        cost_estimate=cost(2 * items * rows * width * 3 * cols, 8 * width * cols * 2),
        name="project",
    )(offsets, tokens, gain[None], shift[None], bias, *pieces)


def k_attend(len_ref, q_ref, k_ref, v_ref, c_ref, *, scale):
    rows, width = c_ref.shape
    valid = lax.broadcasted_iota(jnp.int32, (1, rows), 1) < IMG + len_ref[0]
    low = lax.broadcasted_iota(jnp.int32, (1, LANES), 1) < HDIM
    for pair in range(width // LANES):
        cols = slice(pair * LANES, (pair + 1) * LANES)
        q, k, v = q_ref[0, 0, :, cols], k_ref[0, 0, :, cols], v_ref[0, 0, :, cols]
        both = []
        for side in (low, ~low):
            s = dot(q * side.astype(BF), k, NT) * scale
            s = jnp.where(valid, s, -1e30)
            e = jnp.exp(s - jnp.max(s, axis=-1, keepdims=True))
            p = (e / jnp.sum(e, axis=-1, keepdims=True)).astype(BF)
            both.append(dot(p, v, NN))
        c_ref[:, cols] = jnp.where(low, both[0], both[1]).astype(BF)


def attend(item, text_len, qkv, scale):
    _, _, rows, cols = qkv.shape
    spec = [
        pl.BlockSpec((1, 1, rows, cols), lambda i, *_, t=t: (t, item, 0, 0)) for t in range(3)
    ]
    grid_spec = pltpu.PrefetchScalarGridSpec(
        num_scalar_prefetch=1,
        grid=(1,),
        in_specs=spec,
        out_specs=full((rows, cols)),
    )
    return pl.pallas_call(
        functools.partial(k_attend, scale=scale),
        grid_spec=grid_spec,
        out_shape=jax.ShapeDtypeStruct((rows, cols), BF),
        compiler_params=params(),
        cost_estimate=cost(4 * rows * rows * cols * 4, 8 * rows * cols, rows * rows * 6),
        name="attend",
    )(text_len[item : item + 1], qkv, qkv, qkv)


def k_residual(tok_ref, cm_ref, cp_ref, wm_ref, wp_ref, bias_ref, gain_ref, shift_ref, h_ref, b_ref):
    y = dot(cm_ref[...], wm_ref[0], NT) + dot(cp_ref[...], wp_ref[0], NT)
    h = tok_ref[0].astype(F32) + (y + bias_ref[...])
    h_ref[...] = h
    hat, _ = normed(h)
    b_ref[...] = (hat * gain_ref[...] + shift_ref[...]).astype(BF)


def residual(item, tokens, mine, theirs, w_mine, w_theirs, bias, gain, shift):
    _, rows, width = tokens.shape
    cols = mine.shape[1]
    last = w_mine.shape[0] - 1
    return pl.pallas_call(
        k_residual,
        grid=(1,),
        in_specs=[
            pl.BlockSpec((1, rows, width), lambda i: (item, 0, 0)),
            full((rows, cols)),
            full((rows, cols)),
            pl.BlockSpec((1, width, cols), lambda i: (last, 0, 0)),
            full((1, width, cols)),
            full((1, width)),
            full((1, width)),
            full((1, width)),
        ],
        out_specs=[full((rows, width)), full((rows, width))],
        out_shape=[
            jax.ShapeDtypeStruct((rows, width), F32),
            jax.ShapeDtypeStruct((rows, width), BF),
        ],
        compiler_params=params(),
        cost_estimate=cost(4 * rows * cols * width, 10 * rows * width),
        name="residual",
    )(tokens, mine, theirs, w_mine, w_theirs, bias[None], gain[None], shift[None])


def segments(rows):
    head = up_to(IMG, SUB)
    tail = IMG // SUB * SUB
    return (0, head), (tail, rows - tail), head


def segment_masks(rows):
    (a0, an), (b0, bn), _ = segments(rows)
    in_a = lax.broadcasted_iota(jnp.int32, (an, 1), 0) + a0 < IMG
    in_b = lax.broadcasted_iota(jnp.int32, (bn, 1), 0) + b0 >= IMG
    return in_a, in_b


def masked_parts(g_ref):
    rows = g_ref.shape[1]
    (a0, an), (b0, bn), _ = segments(rows)
    in_a, in_b = segment_masks(rows)
    g_a = jnp.where(in_a, g_ref[0, a0 : a0 + an, :].astype(F32), 0.0)
    g_b = jnp.where(in_b, g_ref[0, b0 : b0 + bn, :].astype(F32), 0.0)
    return g_a, g_b


def write_chunks(slot_ref, acc_ref, outs):
    _, total, width = acc_ref.shape
    count = sum(o.shape[0] for o in outs)
    rows = total // count
    per = outs[0].shape[0]
    for c in range(count):
        slot = slot_ref[c]
        for n, out in enumerate(outs):

            @pl.when((slot >= n * per) & (slot < (n + 1) * per))
            def _(out=out, n=n):
                out[slot - n * per] = acc_ref[:, c * rows : (c + 1) * rows, :].astype(BF)


def k_up(e_ref, off_ref, slot_ref, b_ref, g_ref, bias_ref, *rest, n_out, own):
    scratch = rest[-3:]
    w_s, dw_s, sems = scratch
    outs = rest[-3 - n_out - 3 : -3]
    act_ref, slope_ref, gbd_ref = outs[:3]
    dw_refs = outs[3:]
    pieces = rest[: -3 - n_out - 3]
    i = pl.program_id(0)

    @pl.when(i == 0)
    def _():
        for c in place_copies(off_ref, pieces, w_s, sems):
            c.start()
        dw_s[...] = jnp.zeros_like(dw_s)
        gbd_ref[...] = jnp.zeros_like(gbd_ref)
        for c in place_copies(off_ref, pieces, w_s, sems):
            c.wait()

    rows = b_ref.shape[1]
    seg_a, seg_b, head = segments(rows)
    at = 0
    for which, (lo, n), g in zip((0, 1), (seg_a, seg_b), masked_parts(g_ref)):
        e = e_ref[which, i]
        u = dot(b_ref[0, lo : lo + n, :], w_s[e], NN) + bias_ref[pl.ds(e, 1), :]
        cdf = 0.5 * (1.0 + lax.erf(u * ROOT_HALF))
        act = (u * cdf).astype(BF)
        act_ref[0, at : at + n, :] = act
        slope_ref[0, at : at + n, :] = (cdf + u * jnp.exp(-0.5 * u * u) * INV_ROOT_TAU).astype(BF)
        dw_s[e] += dot(g.astype(BF), act, TN)

        @pl.when(i < own)
        def _(g=g, e=e):
            gbd_ref[pl.ds(e, 1), :] += jnp.sum(g, axis=0, keepdims=True)

        at += n

    @pl.when(i == pl.num_programs(0) - 1)
    def _():
        write_chunks(slot_ref, dw_s, dw_refs)


def chunk_outs(chunks):
    return [full(c) for c in chunks], [jax.ShapeDtypeStruct(c, BF) for c in chunks]


def experts_up(experts, offsets, slots, b, g, bias, pieces, chunks, own):
    items, rows, width = b.shape
    e_count, _, hidden = pieces[0].shape[1:]
    count = len(pieces) * pieces[0].shape[0]
    (_, an), (_, bn), _ = segments(rows)
    chunk_specs, chunk_shapes = chunk_outs(chunks)
    grid_spec = pltpu.PrefetchScalarGridSpec(
        num_scalar_prefetch=3,
        grid=(items,),
        in_specs=[per_item((1, rows, width)), per_item((1, rows, width)), full((e_count, hidden))]
        + [ANY] * len(pieces),
        out_specs=[
            per_item((1, an + bn, hidden)),
            per_item((1, an + bn, hidden)),
            full((e_count, width)),
        ]
        + chunk_specs,
        scratch_shapes=[
            pltpu.VMEM((e_count, width, hidden), BF),
            pltpu.VMEM((e_count, width, hidden), F32),
            pltpu.SemaphoreType.DMA((count,)),
        ],
    )
    return pl.pallas_call(
        functools.partial(k_up, n_out=len(chunks), own=own),
        grid_spec=grid_spec,
        out_shape=[
            jax.ShapeDtypeStruct((items, an + bn, hidden), BF),
            jax.ShapeDtypeStruct((items, an + bn, hidden), BF),
            jax.ShapeDtypeStruct((e_count, width), F32),
        ]
        + chunk_shapes,
        compiler_params=params(),
        cost_estimate=cost(
            4 * items * rows * width * hidden, 8 * e_count * width * hidden, items * rows * hidden
        ),
        name="experts_up",
    )(experts, offsets, slots, b, g, bias, *pieces)


def k_back(e_ref, off_ref, g_ref, slope_ref, *rest, n_up):
    w_up, w_down, sem_up, sem_down = rest[-4:]
    du_ref, db_ref, gbu_ref = rest[-7:-4]
    ups, downs = rest[:n_up], rest[n_up:-7]
    i = pl.program_id(0)

    @pl.when(i == 0)
    def _():
        for c in place_copies(off_ref, downs, w_down, sem_down):
            c.start()
        for c in place_copies(off_ref, ups, w_up, sem_up):
            c.start()
        gbu_ref[...] = jnp.zeros_like(gbu_ref)
        for c in place_copies(off_ref, downs, w_down, sem_down):
            c.wait()
        for c in place_copies(off_ref, ups, w_up, sem_up):
            c.wait()

    rows = g_ref.shape[1]
    seg_a, seg_b, head = segments(rows)
    tail = seg_b[0]
    at = 0
    both = []
    for which, (lo, n), g in zip((0, 1), (seg_a, seg_b), masked_parts(g_ref)):
        e = e_ref[which, i]
        dact = dot(g.astype(BF), w_down[e], NN)
        du = (dact * slope_ref[0, at : at + n, :].astype(F32)).astype(BF)
        du_ref[0, at : at + n, :] = du
        gbu_ref[pl.ds(e, 1), :] += jnp.sum(du.astype(F32), axis=0, keepdims=True)
        both.append(dot(du, w_up[e], NT))
        at += n
    db_ref[0, :tail, :] = both[0][:tail].astype(BF)
    db_ref[0, tail:head, :] = (both[0][tail:] + both[1][: head - tail]).astype(BF)
    db_ref[0, head:, :] = both[1][head - tail :].astype(BF)


def experts_back(experts, offsets, g, slope, ups, downs):
    items, rows, width = g.shape
    e_count, _, hidden = ups[0].shape[1:]
    count = len(ups) * ups[0].shape[0]
    seg_rows = slope.shape[1]
    grid_spec = pltpu.PrefetchScalarGridSpec(
        num_scalar_prefetch=2,
        grid=(items,),
        in_specs=[per_item((1, rows, width)), per_item((1, seg_rows, hidden))]
        + [ANY] * (len(ups) + len(downs)),
        out_specs=[
            per_item((1, seg_rows, hidden)),
            per_item((1, rows, width)),
            full((e_count, hidden)),
        ],
        scratch_shapes=[
            pltpu.VMEM((e_count, width, hidden), BF),
            pltpu.VMEM((e_count, width, hidden), BF),
            pltpu.SemaphoreType.DMA((count,)),
            pltpu.SemaphoreType.DMA((count,)),
        ],
    )
    return pl.pallas_call(
        functools.partial(k_back, n_up=len(ups)),
        grid_spec=grid_spec,
        out_shape=[
            jax.ShapeDtypeStruct((items, seg_rows, hidden), BF),
            jax.ShapeDtypeStruct((items, rows, width), BF),
            jax.ShapeDtypeStruct((e_count, hidden), F32),
        ],
        compiler_params=params(),
        cost_estimate=cost(4 * items * rows * width * hidden, 8 * e_count * width * hidden),
        name="experts_back",
    )(experts, offsets, g, slope, *ups, *downs)


def k_up_grad(e_ref, slot_ref, b_ref, du_ref, *rest):
    dw_s = rest[-1]
    dw_refs = rest[:-1]
    i = pl.program_id(0)

    @pl.when(i == 0)
    def _():
        dw_s[...] = jnp.zeros_like(dw_s)

    seg_a, seg_b, _ = segments(b_ref.shape[1])
    at = 0
    for which, (lo, n) in zip((0, 1), (seg_a, seg_b)):
        e = e_ref[which, i]
        dw_s[e] += dot(b_ref[0, lo : lo + n, :], du_ref[0, at : at + n, :], TN)
        at += n

    @pl.when(i == pl.num_programs(0) - 1)
    def _():
        write_chunks(slot_ref, dw_s, dw_refs)


def experts_up_grad(experts, slots, b, du, chunks, e_count):
    items, rows, width = b.shape
    seg_rows, hidden = du.shape[1:]
    chunk_specs, chunk_shapes = chunk_outs(chunks)
    grid_spec = pltpu.PrefetchScalarGridSpec(
        num_scalar_prefetch=2,
        grid=(items,),
        in_specs=[per_item((1, rows, width)), per_item((1, seg_rows, hidden))],
        out_specs=chunk_specs,
        scratch_shapes=[pltpu.VMEM((e_count, width, hidden), F32)],
    )
    return pl.pallas_call(
        k_up_grad,
        grid_spec=grid_spec,
        out_shape=chunk_shapes,
        compiler_params=params(),
        cost_estimate=cost(2 * items * rows * width * hidden, 4 * e_count * width * hidden),
        name="experts_up_grad",
    )(experts, slots, b, du)


def k_down(e_ref, off_ref, act_ref, *rest):
    z_ref, w_down, sems = rest[-3:]
    pieces = rest[:-3]
    i = pl.program_id(0)

    @pl.when(i == 0)
    def _():
        for c in place_copies(off_ref, pieces, w_down, sems):
            c.start()
        for c in place_copies(off_ref, pieces, w_down, sems):
            c.wait()

    rows = z_ref.shape[1]
    seg_a, seg_b, head = segments(rows)
    tail = seg_b[0]
    z_a = dot(act_ref[0, : seg_a[1], :], w_down[e_ref[0, i]], NT)
    z_b = dot(act_ref[0, seg_a[1] :, :], w_down[e_ref[1, i]], NT)
    image = lax.broadcasted_iota(jnp.int32, (head - tail, 1), 0) + tail < IMG
    z_ref[0, :tail, :] = z_a[:tail].astype(BF)
    z_ref[0, tail:head, :] = jnp.where(image, z_a[tail:], z_b[: head - tail]).astype(BF)
    z_ref[0, head:, :] = z_b[head - tail :].astype(BF)


def experts_down(experts, offsets, act, pieces, rows):
    items, seg_rows, hidden = act.shape
    e_count = pieces[0].shape[1]
    width = sum(p.shape[0] * p.shape[2] for p in pieces)
    count = len(pieces) * pieces[0].shape[0]
    grid_spec = pltpu.PrefetchScalarGridSpec(
        num_scalar_prefetch=2,
        grid=(items,),
        in_specs=[per_item((1, seg_rows, hidden))] + [ANY] * len(pieces),
        out_specs=per_item((1, rows, width)),
        scratch_shapes=[
            pltpu.VMEM((e_count, width, hidden), BF),
            pltpu.SemaphoreType.DMA((count,)),
        ],
    )
    return pl.pallas_call(
        k_down,
        grid_spec=grid_spec,
        out_shape=jax.ShapeDtypeStruct((items, rows, width), BF),
        compiler_params=params(),
        cost_estimate=cost(2 * items * rows * width * hidden, 4 * e_count * width * hidden),
        name="experts_down",
    )(experts, offsets, act, *pieces)


def k_output(e_ref, h_ref, zm_ref, zp_ref, bias_ref, o_ref):
    i = pl.program_id(0)
    rows, keep = h_ref.shape[1], o_ref.shape[1]
    image = lax.broadcasted_iota(jnp.int32, (rows, 1), 0) < IMG
    bias = jnp.where(image, bias_ref[pl.ds(e_ref[0, i], 1), :], bias_ref[pl.ds(e_ref[1, i], 1), :])
    out = h_ref[0] + ((zm_ref[0].astype(F32) + zp_ref[0].astype(F32)) + bias)
    o_ref[0] = out[:keep].astype(BF)


def finish_output(experts, h, mine, theirs, bias, keep):
    items, rows, width = h.shape
    grid_spec = pltpu.PrefetchScalarGridSpec(
        num_scalar_prefetch=1,
        grid=(items,),
        in_specs=[per_item((1, rows, width))] * 3 + [full(bias.shape)],
        out_specs=per_item((1, keep, width)),
    )
    return pl.pallas_call(
        k_output,
        grid_spec=grid_spec,
        out_shape=jax.ShapeDtypeStruct((items, keep, width), BF),
        compiler_params=params(),
        cost_estimate=cost(8 * items * rows * width, 10 * items * rows * width),
        name="finish_output",
    )(experts, h, mine, theirs, bias)


def k_attend_back(
    len_ref, dm_ref, dp_ref, h_ref, g_ref, tok_ref, q_ref, k_ref, v_ref, w_ref, fgain_ref, again_ref,
    dh_ref, dy_ref, dqkv_ref, da_ref, sums_ref, bias_ref, *, scale,
):
    rows, width = dh_ref.shape
    cols = q_ref.shape[3]
    db = dm_ref[...].astype(F32) + dp_ref[...].astype(F32)
    hat, spread = normed(h_ref[...])
    dh = g_ref[0].astype(F32) + norm_back(db, hat, spread, fgain_ref[...])
    dh_ref[...] = dh
    dy = dh.astype(BF)
    dy_ref[...] = dy
    sums_ref[0:1, :] = jnp.sum(db * hat, axis=0, keepdims=True)
    sums_ref[1:2, :] = jnp.sum(db, axis=0, keepdims=True)
    sums_ref[2:3, :] = jnp.sum(dy.astype(F32), axis=0, keepdims=True)
    dctx = dot(dy, w_ref[3], NN).astype(BF)
    valid = lax.broadcasted_iota(jnp.int32, (rows, 1), 0) < IMG + len_ref[0]
    low = lax.broadcasted_iota(jnp.int32, (1, LANES), 1) < HDIM
    for pair in range(cols // LANES):
        at = slice(pair * LANES, (pair + 1) * LANES)
        q, k, v = q_ref[0, 0, :, at], k_ref[0, 0, :, at], v_ref[0, 0, :, at]
        dc = dctx[:, at]
        parts = []
        for side in (low, ~low):
            only = side.astype(BF)
            s = dot(k * only, q, NT) * scale
            s = jnp.where(valid, s, -1e30)
            e = jnp.exp(s - jnp.max(s, axis=0, keepdims=True))
            p = e / jnp.sum(e, axis=0, keepdims=True)
            dp = dot(v * only, dc, NT)
            ds = (p * (dp - jnp.sum(p * dp, axis=0, keepdims=True))).astype(BF)
            parts.append((dot(ds, k, TN), dot(ds, q, NN), dot(p.astype(BF), dc, NN)))
        dqkv_ref[0, :, at] = (jnp.where(low, parts[0][0], parts[1][0]) * scale).astype(BF)
        dqkv_ref[1, :, at] = (jnp.where(low, parts[0][1], parts[1][1]) * scale).astype(BF)
        dqkv_ref[2, :, at] = jnp.where(low, parts[0][2], parts[1][2]).astype(BF)
    da = dot(dqkv_ref[0], w_ref[0], NT)
    da += dot(dqkv_ref[1], w_ref[1], NT)
    da += dot(dqkv_ref[2], w_ref[2], NT)
    bias_ref[0:1, :] = jnp.sum(dqkv_ref[0].astype(F32), axis=0, keepdims=True)
    bias_ref[1:2, :] = jnp.sum(dqkv_ref[2].astype(F32), axis=0, keepdims=True)
    hat, _ = normed(tok_ref[0].astype(F32))
    sums_ref[3:4, :] = jnp.sum(da * hat, axis=0, keepdims=True)
    sums_ref[4:5, :] = jnp.sum(da, axis=0, keepdims=True)
    da_ref[...] = da.astype(BF)


def attend_back(item, text_len, mine, theirs, h, g, tokens, qkv, weights, ffn_gain, attn_gain, scale):
    rows, width = h.shape
    cols = qkv.shape[3]
    item_spec = pl.BlockSpec((1, rows, width), lambda i, *_: (item, 0, 0))
    grid_spec = pltpu.PrefetchScalarGridSpec(
        num_scalar_prefetch=1,
        grid=(1,),
        in_specs=[full((rows, width))] * 3
        + [item_spec, item_spec]
        + [pl.BlockSpec((1, 1, rows, cols), lambda i, *_, t=t: (t, item, 0, 0)) for t in range(3)]
        + [full(weights.shape), full((1, width)), full((1, width))],
        out_specs=[
            full((rows, width)),
            full((rows, width)),
            full((3, rows, cols)),
            full((rows, width)),
            full((5, width)),
            full((2, cols)),
        ],
    )
    return pl.pallas_call(
        functools.partial(k_attend_back, scale=scale),
        grid_spec=grid_spec,
        out_shape=[
            jax.ShapeDtypeStruct((rows, width), F32),
            jax.ShapeDtypeStruct((rows, width), BF),
            jax.ShapeDtypeStruct((3, rows, cols), BF),
            jax.ShapeDtypeStruct((rows, width), BF),
            jax.ShapeDtypeStruct((5, width), F32),
            jax.ShapeDtypeStruct((2, cols), F32),
        ],
        compiler_params=params(),
        cost_estimate=cost(
            8 * rows * cols * width + 20 * rows * rows * cols, 30 * rows * width, rows * rows * 6
        ),
        name="attend_back",
    )(
        text_len[item : item + 1], mine, theirs, h, g, tokens, qkv, qkv, qkv, weights,
        ffn_gain[None], attn_gain[None],
    )


def k_attn_grad(slot_ref, *rest, items, n_out):
    acc = rest[-1]
    outs = rest[-1 - n_out : -1]
    a_refs, d_refs = rest[:items], rest[items : 2 * items]
    y_refs, c_refs = rest[2 * items : 3 * items], rest[3 * items : 4 * items]
    for n in range(items):
        for t in range(4):
            left, right = (a_refs[n][0], d_refs[n][t]) if t < 3 else (y_refs[n][...], c_refs[n][...])
            part = dot(left, right, TN)
            if n == 0:
                acc[t] = part
            else:
                acc[t] += part
    write_chunks(slot_ref, acc, outs)


def attn_grad(slots, a, dqkv, dy, ctx, chunks):
    items, rows, width = a.shape
    cols = ctx[0].shape[1]
    chunk_specs, chunk_shapes = chunk_outs(chunks)
    grid_spec = pltpu.PrefetchScalarGridSpec(
        num_scalar_prefetch=1,
        grid=(1,),
        in_specs=[
            pl.BlockSpec((1, rows, width), lambda i, *_, n=n: (n, 0, 0)) for n in range(items)
        ]
        + [full((3, rows, cols))] * items
        + [full((rows, width))] * items
        + [full((rows, cols))] * items,
        out_specs=chunk_specs,
        scratch_shapes=[pltpu.VMEM((4, width, cols), F32)],
    )
    return pl.pallas_call(
        functools.partial(k_attn_grad, items=items, n_out=len(chunks)),
        grid_spec=grid_spec,
        out_shape=chunk_shapes,
        compiler_params=params(),
        cost_estimate=cost(8 * items * rows * width * cols, 16 * width * cols),
        name="attn_grad",
    )(slots, *([a] * items), *dqkv, *dy, *ctx)


def k_token_grad(dh_ref, dm_ref, dp_ref, tok_ref, gain_ref, buf_ref, o_ref):
    del buf_ref
    keep = o_ref.shape[1]
    da = dm_ref[...].astype(F32) + dp_ref[...].astype(F32)
    hat, spread = normed(tok_ref[0].astype(F32))
    out = dh_ref[...] + norm_back(da, hat, spread, gain_ref[...])
    o_ref[0] = out[:keep]


def token_grad(item, dh, mine, theirs, tokens, gain, buffer):
    rows, width = dh.shape
    keep = buffer.shape[1]
    return pl.pallas_call(
        k_token_grad,
        grid=(1,),
        in_specs=[full((rows, width))] * 3
        + [pl.BlockSpec((1, rows, width), lambda i: (item, 0, 0)), full((1, width)), ANY],
        out_specs=pl.BlockSpec((1, keep, width), lambda i: (item, 0, 0)),
        out_shape=jax.ShapeDtypeStruct(buffer.shape, F32),
        input_output_aliases={5: 0},
        compiler_params=params(),
        cost_estimate=cost(10 * rows * width, 14 * rows * width),
        name="token_grad",
    )(dh, mine, theirs, tokens, gain[None], buffer)


def swap(value, axis, size, mask):
    return lax.ppermute(value, axis, [(i, i ^ mask) for i in range(size)])


def spread_pieces(own, masks, size):
    held = [(0, own)]
    for mask in masks:
        held = held + [(r | mask, swap(piece, "dp", size, mask)) for r, piece in held]
    return held


def after(value, *others):
    return lax.optimization_barrier((value,) + others)[0]


def add_low(a, b):
    return (a.astype(F32) + b.astype(F32)).astype(BF)


def fold_chunks(chunk, masks, size):
    for n, mask in enumerate(masks):
        half = chunk.shape[0] // 2
        got = swap(chunk[half:], "dp", size, mask)
        if n == len(masks) - 1:
            return chunk[:half].astype(F32) + got.astype(F32)
        chunk = add_low(chunk[:half], got)
    return chunk.astype(F32)


def per_device(
    tokens, text_len, routes, attn_gain, attn_shift, w_qkv, b_qv, w_out, b_out, ffn_gain, ffn_shift,
    w_up, b_up, w_down, b_down, cotangent, *, dp, rep,
):
    items, seq, width = tokens.shape
    rows = up_to(seq, SUB)
    share = w_qkv.shape[1]
    cols = w_qkv.shape[2]
    hidden = w_up.shape[2] // 2
    e_count = w_up.shape[0]
    scale = 1.0 / math.sqrt(HDIM)
    me = lax.axis_index("dp")
    core = me % 2
    by_permute = share % SUB == 0
    gather_masks = [m for m in (4, 8, 16, 32, 64, 128) if m < dp] + [2]
    fold_masks = [2] + [m for m in (128, 64, 32, 16, 8, 4) if m < dp]

    def peer(value):
        return lax.ppermute(value, "rep", [(i, i ^ 1) for i in range(rep)])

    def partner(value):
        return swap(value, "dp", dp, 1)

    pad = ((0, 0), (0, rows - seq), (0, 0))
    tok = jnp.pad(tokens, pad)
    cot = jnp.pad(cotangent, pad)

    attn_shard = jnp.concatenate([w_qkv, w_out[None]], axis=0)
    my_half = lax.dynamic_slice_in_dim(w_up, core * hidden, hidden, 2)
    other_half = lax.dynamic_slice_in_dim(w_up, (1 - core) * hidden, hidden, 2)
    my_half_d = lax.dynamic_slice_in_dim(w_down, core * hidden, hidden, 2)
    other_half_d = lax.dynamic_slice_in_dim(w_down, (1 - core) * hidden, hidden, 2)
    if by_permute:
        held = spread_pieces(attn_shard[None], gather_masks, dp)
        held = held + [(r ^ 1, partner(p)) for r, p in held]
        attn_pieces = [p for _, p in held]
        attn_off = jnp.stack([(me ^ r) * share for r, _ in held]).astype(jnp.int32)
        up_own = jnp.stack([my_half, partner(other_half)])
        down_own = jnp.stack([my_half_d, partner(other_half_d)])
        up_own = after(up_own, held[dp // 2 - 1][1])
        up_held = spread_pieces(up_own, gather_masks, dp)
        down_own = after(down_own, up_held[-1][1])
        down_held = spread_pieces(down_own, gather_masks, dp)
        up_pieces, down_pieces = [p for _, p in up_held], [p for _, p in down_held]
        ffn_off = jnp.stack(
            [(me ^ r ^ j) * share for r, _ in up_held for j in (0, 1)]
        ).astype(jnp.int32)
        ids = jnp.arange(dp, dtype=jnp.int32) ^ me.astype(jnp.int32)
        slots = jnp.zeros_like(ids)
        weight = dp // 4
        for m in fold_masks:
            slots = slots + (ids & m) // m * weight
            weight //= 2
        slots = slots + (ids & 1) * (dp // 2)
        ffn_chunks = [(dp // 2, e_count, share, hidden)] * 2
        attn_chunks = [(dp // 2, 4, share, cols)] * 2
    else:
        attn_pieces = [lax.all_gather(attn_shard, "dp", axis=1, tiled=True)[None]]
        gathered = lax.all_gather(w_up, "dp", axis=1, tiled=True)
        up_pieces = [lax.dynamic_slice_in_dim(gathered, core * hidden, hidden, 2)[None]]
        gathered = lax.all_gather(w_down, "dp", axis=1, tiled=True)
        down_pieces = [lax.dynamic_slice_in_dim(gathered, core * hidden, hidden, 2)[None]]
        attn_off = ffn_off = slots = jnp.zeros((1,), jnp.int32)
        ffn_chunks = [(1, e_count, width, hidden)]
        attn_chunks = [(1, 4, width, cols)]

    experts = jnp.stack([routes[:, 0], routes[:, seq - 1]]).astype(jnp.int32)
    experts_two = jnp.concatenate([experts, partner(experts)], axis=1)
    cot_two = jnp.concatenate([cot, partner(cot)], axis=0)

    bias = jnp.stack([b_qv[0], jnp.zeros_like(b_qv[0]), b_qv[1]])
    a, qkv, attn_w = project(tok, attn_gain, attn_shift, bias, attn_pieces, attn_off)
    out_theirs = peer(attn_w[3:])
    ctx, h, b = [], [], []
    for n in range(items):
        ctx.append(attend(n, text_len, qkv, scale))
    ctx_theirs = [peer(c) for c in ctx]
    for n in range(items):
        h_n, b_n = residual(
            n, tok, ctx[n], ctx_theirs[n], attn_w, out_theirs, b_out, ffn_gain, ffn_shift
        )
        h.append(h_n)
        b.append(b_n)
    b_two = jnp.stack(b + [partner(v) for v in b])

    b_up_mine = lax.dynamic_slice_in_dim(b_up, core * hidden, hidden, 1)
    act, slope, grad_b_down, *down_grad = experts_up(
        experts_two, ffn_off, slots, b_two, cot_two, b_up_mine, up_pieces, ffn_chunks, items
    )
    du, db_two, grad_b_up = experts_back(
        experts_two, ffn_off, cot_two, slope, up_pieces, down_pieces
    )
    up_grad = experts_up_grad(experts_two, slots, b_two, du, ffn_chunks, e_count)
    db = [add_low(db_two[n], partner(db_two[items + n])) for n in range(items)]
    db_theirs = [peer(v) for v in db]

    z_two = experts_down(experts_two, ffn_off, act, down_pieces, rows)
    z = add_low(z_two[:items], partner(z_two[items:]))
    output = finish_output(experts, jnp.stack(h), z, peer(z), b_down, seq)

    dh, dy, dqkv, da, sums, bias_sums = [], [], [], [], 0.0, 0.0
    for n in range(items):
        dh_n, dy_n, dqkv_n, da_n, sums_n, bias_n = attend_back(
            n, text_len, db[n], db_theirs[n], h[n], cot, tok, qkv, attn_w, ffn_gain, attn_gain, scale
        )
        dh.append(dh_n)
        dy.append(dy_n)
        dqkv.append(dqkv_n)
        da.append(da_n)
        sums = sums + sums_n
        bias_sums = bias_sums + bias_n
    da_theirs = [peer(v) for v in da]
    attn_parts = attn_grad(slots, a, dqkv, dy, ctx, attn_chunks)
    grad_tokens = jnp.zeros((items, seq, width), F32)
    for n in range(items):
        grad_tokens = token_grad(n, dh[n], da[n], da_theirs[n], tok, attn_gain, grad_tokens)

    if by_permute:

        def finish(chunks):
            other = fold_chunks(chunks[1], fold_masks, dp)[0]
            own = fold_chunks(chunks[0], fold_masks, dp)[0]
            got = partner(other)
            first = core == 0
            return jnp.concatenate(
                [jnp.where(first, own, got), jnp.where(first, got, own)], axis=-1
            )

        grad_w_down = finish(down_grad)
        grad_w_up = finish(up_grad)
        merged = add_low(attn_parts[0], partner(attn_parts[1]))
        grad_attn = fold_chunks(merged, fold_masks, dp)[0]
        grad_w_qkv, grad_w_out = grad_attn[:3], grad_attn[3]
    else:

        def finish(chunk):
            whole = jnp.zeros((e_count, width, 2 * hidden), BF)
            whole = lax.dynamic_update_slice_in_dim(whole, chunk[0], core * hidden, 2)
            return lax.psum_scatter(whole, "dp", scatter_dimension=1, tiled=True).astype(F32)

        grad_w_down, grad_w_up = finish(down_grad[0]), finish(up_grad[0])
        grad_attn = lax.psum_scatter(attn_parts[0][0], "dp", scatter_dimension=1, tiled=True)
        grad_w_qkv, grad_w_out = grad_attn[:3].astype(F32), grad_attn[3].astype(F32)

    first_norm = sums[3:5]
    first_norm = first_norm + peer(first_norm)
    up_pair = jnp.zeros((2, e_count, hidden), F32)
    up_pair = lax.dynamic_update_slice_in_dim(up_pair, grad_b_up[None], core, 0)
    small = jnp.concatenate(
        [
            first_norm.reshape(-1),
            sums[0:3].reshape(-1),
            grad_b_down.reshape(-1),
            up_pair.reshape(-1),
            bias_sums.reshape(-1),
        ]
    ).reshape(-1, LANES)
    for mask in [1] + gather_masks:
        small = small + swap(small, "dp", dp, mask)
    small = small.reshape(-1)
    at = 0

    def take(*shape):
        nonlocal at
        n = math.prod(shape)
        piece = small[at : at + n].reshape(shape)
        at += n
        return piece

    norm_one, norm_two, grad_b_out = take(2, width), take(2, width), take(width)
    total_down = take(e_count, width)
    total_up = jnp.moveaxis(take(2, e_count, hidden), 0, 1).reshape(e_count, 2 * hidden)
    total_qv = take(2, cols)
    return (
        output,
        grad_tokens,
        grad_w_qkv,
        grad_w_out,
        grad_w_up,
        grad_w_down,
        total_qv,
        grad_b_out,
        total_up,
        total_down,
        jnp.concatenate([norm_one, norm_two], axis=0),
    )


def solution(mesh):
    body = functools.partial(per_device, dp=mesh.shape["dp"], rep=mesh.shape["rep"])
    return jax.shard_map(
        body,
        mesh=mesh,
        in_specs=(
            P("dp", None, None),
            P("dp"),
            P("dp", None),
            P(),
            P(),
            P(None, "dp", "rep"),
            P(None, "rep"),
            P("dp", "rep"),
            P(),
            P(),
            P(),
            P(None, "dp", "rep"),
            P(None, "rep"),
            P(None, "dp", "rep"),
            P(),
            P("dp", None, None),
        ),
        out_specs=(
            P("dp", None, None),
            P("dp", None, None),
            P(None, "dp", "rep"),
            P("dp", "rep"),
            P(None, "dp", "rep"),
            P(None, "dp", "rep"),
            P(None, "rep"),
            P(),
            P(None, "rep"),
            P(),
            P(),
        ),
        check_vma=False,
    )
```

time: 1430 us -> 423 us (0.30)
  waiting for transfers between devices: 812 us -> 139 us
  matrix products: 278 us -> 0 us
  Pallas kernels: 0 us -> 137 us
  local copies, waits for them, and re-layouts: 170 us -> 40.4 us
  blocking collectives: 92.4 us -> 0 us
  starting transfers between devices: 0.53 us -> 72.3 us
  other arithmetic: 52.1 us -> 28.2 us
    unnamed x18 -> x0, waiting for transfers between devices: 640 us -> none
    dot_general x24 -> x0, matrix products: 278 us -> none  [the longest x1 67.2 us: per_device(): jnp.einsum('te,tdf->edf', owner_hot, up_projection_terms, precision=HIGHEST)]
    ppermute x0 -> x74, waiting for transfers between devices: none -> 139 us  [the longest x62 125 us: swap(): return lax.ppermute(value, axis, [(i, i ^ mask) for i in range(size)])]
    pallas_call x0 -> x19, Pallas kernels: none -> 137 us  [the longest x3 28.2 us: attend_back(): pl.pallas_call(functools.partial(k_attend_back, scale=scale), grid_spec=g...]
    all_gather x7 -> x0, waiting for transfers between devices: 117 us -> none  [the longest x1 57.5 us: per_device(): lax.all_gather(w_up, 'dp', axis=1, tiled=True)]
    ppermute x0 -> x74, starting transfers between devices: none -> 72.3 us  [the longest x62 59.8 us: swap(): return lax.ppermute(value, axis, [(i, i ^ mask) for i in range(size)])]
    psum x1 -> x0, blocking collectives: 65.4 us -> none  [per_device(): lax.psum((grad_b_qv, grad_b_out, grad_b_up, grad_b_down, norm_local), 'dp')]
    unnamed x128 -> x113, local copies, waits for them, and re-layouts: 67 us -> 8.34 us
  transfers between devices with their start and end apart: 13 -> 74, of which waited for: 8 -> 23; matrix products, arithmetic and copies ran while one was open for 26% -> 14% of each run, Pallas kernels for 0% -> 33%
where the time goes in v1:
time: 423 us; the launch traced here: 419 us
  waiting for transfers between devices  139 us (33%)
  Pallas kernels  137 us (32%)
  starting transfers between devices  72.3 us (17%)
  local copies, waits for them, and re-layouts  40.4 us (10%)
  other arithmetic  28.2 us (7%)
    ppermute x62, waiting for transfers between devices, swap(): return lax.ppermute(value, axis, [(i, i ^ mask) for i in range(size)])  125 us
    ppermute x62, starting transfers between devices, swap(): return lax.ppermute(value, axis, [(i, i ^ mask) for i in range(size)])  59.8 us
    pallas_call x3, Pallas kernels, attend_back(): pl.pallas_call(functools.partial(k_attend_back, scale=scale), grid_spec=g...  28.2 us
    pallas_call x1, Pallas kernels, experts_up(): pl.pallas_call(functools.partial(k_up, n_out=len(chunks), own=own), grid_...  18.4 us
    pallas_call x1, Pallas kernels, experts_back(): pl.pallas_call(functools.partial(k_back, n_up=len(ups)), grid_spec=grid_s...  14.3 us
    ppermute x12, waiting for transfers between devices, peer(): return lax.ppermute(value, 'rep', [(i, i ^ 1) for i in range(rep)])  13.8 us
    pallas_call x3, Pallas kernels, attend(): pl.pallas_call(functools.partial(k_attend, scale=scale), grid_spec=grid_s...  13.2 us
    convert_element_type x13, other arithmetic, add_low(): return (a.astype(F32) + b.astype(F32)).astype(BF)  12.6 us
  transfers between devices with their start and end apart: 74, of which 23 were waited for; matrix products, arithmetic and copies ran while one was open for 14% of the time, Pallas kernels for 33%

profile of v1, /device:TPU:0, one launch (start us, length us, event | category | flops | bytes accessed | tf_op | source)
XLA Modules:
  0.0 419.1 jit_solution(15524691673418642484)
XLA Ops:
  34.8 8.6 %project.1 = (bf16[3,272,768]{2,1,0:T(8,128)(2,1)}, bf16[3,3,272,384]{3,2,1,0:T(8,128)(2,1)}, bf16[4,768,384]{2,1,0:T(8,128)(2,1)}) custom-call(s32[16]{0:T(128)} %stack.158.off_ref, bf16[3,272,768]{2,1,0:T(8,128)(2,1)} %pad.7.tok_ref, f32[1,768]{1,0:T(1,128)} %broadcast_in_dim.20.gain_ref.again_ref, f32[1,768]{1,0:T(1,128)} %broadcast_in_dim.21.shift_ref, ...), custom_call_target="tpu_custom_call" | custom-call | flops 1443889152 | bytes 4718592 | tf_op jit(solution)/shard_map/project/pallas_call | solution.py:131
  54.5 4.4 %attend.4.cm_ref.rest_10_ = bf16[272,384]{1,0:T(8,128)(2,1)} custom-call(s32[1]{0:T(128)} %get-tuple-element.117.len_ref, bf16[3,3,272,384]{3,2,1,0:T(8,128)(2,1)} %get-tuple-element.52.q_ref.k_ref.v_ref, bf16[3,3,272,384]{3,2,1,0:T(8,128)(2,1)} %get-tuple-element.52.q_ref.k_ref.v_ref, bf16[3,3,272,384]{3,2,1,0:T(8,128)(2,1)} %get-tuple-element.52.q_ref.k_ref.v_ref), custom_call_target="tpu_custom_call" | custom-call | flops 454557696 | bytes 835584 | tf_op jit(solution)/shard_map/attend/pallas_call | solution.py:173
  59.0 4.4 %attend.3.cm_ref.rest_9_ = bf16[272,384]{1,0:T(8,128)(2,1)} custom-call(s32[1]{0:T(128)} %get-tuple-element.115.len_ref, bf16[3,3,272,384]{3,2,1,0:T(8,128)(2,1)} %get-tuple-element.52.q_ref.k_ref.v_ref, bf16[3,3,272,384]{3,2,1,0:T(8,128)(2,1)} %get-tuple-element.52.q_ref.k_ref.v_ref, bf16[3,3,272,384]{3,2,1,0:T(8,128)(2,1)} %get-tuple-element.52.q_ref.k_ref.v_ref), custom_call_target="tpu_custom_call" | custom-call | flops 454557696 | bytes 835584 | tf_op jit(solution)/shard_map/attend/pallas_call | solution.py:173
  90.0 9.6 %collective-permute-done.26.rest_2_ = bf16[2,3,48,768]{3,2,1,0:T(8,128)(2,1)} collective-permute-done((bf16[2,3,48,768]{3,2,1,0:T(8,128)(2,1)}, bf16[2,3,48,768]{3,2,1,0:T(8,128)(2,1)}, u32[]{:S(2)}, u32[]{:S(2)}) %collective-permute-start.26) | collective-permute-done | bytes 442400 | tf_op jit(solution)/shard_map/ppermute | solution.py:686
  100.7 6.7 %collective-permute-done.27.rest_3_ = bf16[2,3,48,768]{3,2,1,0:T(8,128)(2,1)} collective-permute-done((bf16[2,3,48,768]{3,2,1,0:T(8,128)(2,1)}, bf16[2,3,48,768]{3,2,1,0:T(8,128)(2,1)}, u32[]{:S(2)}, u32[]{:S(2)}) %collective-permute-start.27) | collective-permute-done | bytes 442400 | tf_op jit(solution)/shard_map/ppermute | solution.py:686
  111.0 16.6 %collective-permute-done.31.rest_7_ = bf16[2,3,48,768]{3,2,1,0:T(8,128)(2,1)S(1)} collective-permute-done((bf16[2,3,48,768]{3,2,1,0:T(8,128)(2,1)}, bf16[2,3,48,768]{3,2,1,0:T(8,128)(2,1)S(1)}, u32[]{:S(2)}, u32[]{:S(2)}) %collective-permute-start.31) | collective-permute-done | bytes 442400 | tf_op jit(solution)/shard_map/ppermute | solution.py:686
  130.6 18.4 %experts_up.1 = (bf16[6,288,768]{2,1,0:T(8,128)(2,1)}, bf16[6,288,768]{2,1,0:T(8,128)(2,1)}, f32[3,768]{1,0:T(4,128)}, bf16[8,3,48,768]{3,2,1,0:T(8,128)(2,1)}, bf16[8,3,48,768]{3,2,1,0:T(8,128)(2,1)}) custom-call(s32[2,6]{1,0:T(2,128)} %pad_add_fusion.1.e_ref, s32[16]{0:T(128)} %stack.171.off_ref, s32[16]{0:T(128)} %multiply_add_fusion.slot_ref, ...), custom_call_target="tpu_custom_call" | custom-call | flops 3850371072 | bytes 14155776 | tf_op jit(solution)/shard_map/experts_up/pallas_call | solution.py:323
  161.7 24.8 %collective-permute-done.34.rest_2_.rest_10_ = bf16[2,3,48,768]{3,2,1,0:T(8,128)(2,1)} collective-permute-done((bf16[2,3,48,768]{3,2,1,0:T(8,128)(2,1)S(1)}, bf16[2,3,48,768]{3,2,1,0:T(8,128)(2,1)}, u32[]{:S(2)}, u32[]{:S(2)}) %collective-permute-start.34) | collective-permute-done | bytes 442400 | tf_op jit(solution)/shard_map/ppermute | solution.py:686
  187.7 8.2 %collective-permute-done.35.rest_3_.rest_11_ = bf16[2,3,48,768]{3,2,1,0:T(8,128)(2,1)} collective-permute-done((bf16[2,3,48,768]{3,2,1,0:T(8,128)(2,1)}, bf16[2,3,48,768]{3,2,1,0:T(8,128)(2,1)}, u32[]{:S(2)}, u32[]{:S(2)}) %collective-permute-start.35) | collective-permute-done | bytes 442400 | tf_op jit(solution)/shard_map/ppermute | solution.py:686
  206.0 6.1 %collective-permute-done.37.rest_5_.rest_13_ = bf16[2,3,48,768]{3,2,1,0:T(8,128)(2,1)} collective-permute-done((bf16[2,3,48,768]{3,2,1,0:T(8,128)(2,1)}, bf16[2,3,48,768]{3,2,1,0:T(8,128)(2,1)}, u32[]{:S(2)}, u32[]{:S(2)}) %collective-permute-start.37) | collective-permute-done | bytes 442400 | tf_op jit(solution)/shard_map/ppermute | solution.py:686
  212.1 9.5 %collective-permute-done.38.rest_6_.rest_14_ = bf16[2,3,48,768]{3,2,1,0:T(8,128)(2,1)} collective-permute-done((bf16[2,3,48,768]{3,2,1,0:T(8,128)(2,1)}, bf16[2,3,48,768]{3,2,1,0:T(8,128)(2,1)}, u32[]{:S(2)}, u32[]{:S(2)}) %collective-permute-start.38) | collective-permute-done | bytes 442400 | tf_op jit(solution)/shard_map/ppermute | solution.py:686
  221.5 7.4 %collective-permute-done.39.rest_7_.rest_15_ = bf16[2,3,48,768]{3,2,1,0:T(8,128)(2,1)} collective-permute-done((bf16[2,3,48,768]{3,2,1,0:T(8,128)(2,1)}, bf16[2,3,48,768]{3,2,1,0:T(8,128)(2,1)}, u32[]{:S(2)}, u32[]{:S(2)}) %collective-permute-start.39) | collective-permute-done | bytes 442400 | tf_op jit(solution)/shard_map/ppermute | solution.py:686
  228.9 14.3 %experts_back.1 = (bf16[6,288,768]{2,1,0:T(8,128)(2,1)}, bf16[6,272,768]{2,1,0:T(8,128)(2,1)}, f32[3,768]{1,0:T(4,128)}) custom-call(s32[2,6]{1,0:T(2,128)} %pad_add_fusion.1.e_ref, s32[16]{0:T(128)} %stack.171.off_ref, bf16[6,272,768]{2,1,0:T(8,128)(2,1)} %pad_maximum_fusion.1.g_ref, bf16[6,288,768]{2,1,0:T(8,128)(2,1)} %get-tuple-element.63.slope_ref, ...), custom_call_target="tpu_custom_call" | custom-call | flops 3850371072 | bytes 14155776 | tf_op jit(solution)/shard_map/experts_back/pallas_call | solution.py:398
  246.1 10.5 %experts_down.1 = bf16[6,272,768]{2,1,0:T(8,128)(2,1)} custom-call(s32[2,6]{1,0:T(2,128)} %pad_add_fusion.1.e_ref, s32[16]{0:T(128)} %stack.171.off_ref, bf16[6,288,768]{2,1,0:T(8,128)(2,1)} %get-tuple-element.61.act_ref, bf16[2,3,48,768]{3,2,1,0:T(8,128)(2,1)} %copy-done.13, bf16[2,3,48,768]{3,2,1,0:T(8,128)(2,1)} %collective-permute-done.33.rest_1_.rest_9_, ...), custom_call_target="tpu_custom_call" | custom-call | flops 1925185536 | bytes 7077888 | tf_op jit(solution)/shard_map/experts_down/pallas_call | solution.py:492
  267.0 10.8 %experts_up_grad.1 = (bf16[8,3,48,768]{3,2,1,0:T(8,128)(2,1)}, bf16[8,3,48,768]{3,2,1,0:T(8,128)(2,1)}) custom-call(s32[2,6]{1,0:T(2,128)} %pad_add_fusion.1.e_ref, s32[16]{0:T(128)} %multiply_add_fusion.slot_ref, bf16[6,272,768]{2,1,0:T(8,128)(2,1)} %copy-done.31, bf16[6,288,768]{2,1,0:T(8,128)(2,1)} %get-tuple-element.80.du_ref), custom_call_target="tpu_custom_call" | custom-call | flops 1925185536 | bytes 7077888 | tf_op jit(solution)/shard_map/experts_up_grad/pallas_call | solution.py:444
  283.5 9.3 %attend_back.3 = (f32[272,768]{1,0:T(8,128)}, bf16[272,768]{1,0:T(8,128)(2,1)}, bf16[3,272,384]{2,1,0:T(8,128)(2,1)}, bf16[272,768]{1,0:T(8,128)(2,1)}, f32[5,768]{1,0:T(8,128)}, /*index=5*/f32[2,384]{1,0:T(2,128)}) custom-call(s32[1]{0:T(128)} %get-tuple-element.116.len_ref, bf16[272,768]{1,0:T(8,128)(2,1)} %copy-done.16, ...), custom_call_target="tpu_custom_call" | custom-call | flops 1209925632 | bytes 6266880 | tf_op jit(solution)/shard_map/attend_back/pallas_call | solution.py:595
  293.1 9.4 %attend_back.4 = (f32[272,768]{1,0:T(8,128)}, bf16[272,768]{1,0:T(8,128)(2,1)}, bf16[3,272,384]{2,1,0:T(8,128)(2,1)}, bf16[272,768]{1,0:T(8,128)(2,1)}, f32[5,768]{1,0:T(8,128)}, /*index=5*/f32[2,384]{1,0:T(2,128)}) custom-call(s32[1]{0:T(128)} %get-tuple-element.117.len_ref, bf16[272,768]{1,0:T(8,128)(2,1)} %copy-done.15, ...), custom_call_target="tpu_custom_call" | custom-call | flops 1209925632 | bytes 6266880 | tf_op jit(solution)/shard_map/attend_back/pallas_call | solution.py:595
  303.3 9.5 %attend_back.5 = (f32[272,768]{1,0:T(8,128)}, bf16[272,768]{1,0:T(8,128)(2,1)}, bf16[3,272,384]{2,1,0:T(8,128)(2,1)}, bf16[272,768]{1,0:T(8,128)(2,1)}, f32[5,768]{1,0:T(8,128)}, /*index=5*/f32[2,384]{1,0:T(2,128)}) custom-call(s32[1]{0:T(128)} %get-tuple-element.115.len_ref, bf16[272,768]{1,0:T(8,128)(2,1)} %copy-done.14, bf16[272,768]{1,0:T(8,128)(2,1)} %copy-done.27, ...), custom_call_target="tpu_custom_call" | custom-call | flops 1209925632 | bytes 6266880 | tf_op jit(solution)/shard_map/attend_back/pallas_call | solution.py:595
  321.7 9.6 %attn_grad.1 = (bf16[8,4,48,384]{3,2,1,0:T(8,128)(2,1)}, bf16[8,4,48,384]{3,2,1,0:T(8,128)(2,1)}) custom-call(s32[16]{0:T(128)} %multiply_add_fusion.slot_ref, bf16[3,272,768]{2,1,0:T(8,128)(2,1)} %get-tuple-element.71.rest_0_.rest_1_.rest_2_, bf16[3,272,768]{2,1,0:T(8,128)(2,1)} %get-tuple-element.71.rest_0_.rest_1_.rest_2_, ...), custom_call_target="tpu_custom_call" | custom-call | flops 1925185536 | bytes 4718592 | tf_op jit(solution)/shard_map/attn_grad/pallas_call | solution.py:649
  354.0 5.1 %collective-permute-done.47.dp_ref = bf16[272,768]{1,0:T(8,128)(2,1)} collective-permute-done((bf16[272,768]{1,0:T(8,128)(2,1)}, bf16[272,768]{1,0:T(8,128)(2,1)}, u32[]{:S(2)}, u32[]{:S(2)}) %collective-permute-start.47) | collective-permute-done | bytes 417824 | tf_op jit(solution)/shard_map/ppermute | solution.py:732
  373.3 9.0 %collective-permute-done.60 = bf16[1,3,48,768]{3,2,1,0:T(8,128)(2,1)S(1)} collective-permute-done((bf16[1,3,48,768]{3,2,1,0:T(8,128)(2,1)S(1)}, bf16[1,3,48,768]{3,2,1,0:T(8,128)(2,1)S(1)}, u32[]{:S(2)}, u32[]{:S(2)}) %collective-permute-start.60) | collective-permute-done | bytes 221216 | tf_op jit(solution)/shard_map/ppermute | solution.py:686
  383.3 5.2 %collective-permute-done.56 = bf16[2,3,48,768]{3,2,1,0:T(8,128)(2,1)S(1)} collective-permute-done((bf16[2,3,48,768]{3,2,1,0:T(8,128)(2,1)}, bf16[2,3,48,768]{3,2,1,0:T(8,128)(2,1)S(1)}, u32[]{:S(2)}, u32[]{:S(2)}) %collective-permute-start.56) | collective-permute-done | bytes 442400 | tf_op jit(solution)/shard_map/ppermute | solution.py:686
  392.1 8.6 %collective-permute-done.57 = bf16[1,3,48,768]{3,2,1,0:T(8,128)(2,1)S(1)} collective-permute-done((bf16[1,3,48,768]{3,2,1,0:T(8,128)(2,1)S(1)}, bf16[1,3,48,768]{3,2,1,0:T(8,128)(2,1)S(1)}, u32[]{:S(2)}, u32[]{:S(2)}) %collective-permute-start.57) | collective-permute-done | bytes 221216 | tf_op jit(solution)/shard_map/ppermute | solution.py:686
  412.4 5.1 %finish_output.1 = bf16[3,261,768]{2,1,0:T(8,128)(2,1)} custom-call(s32[2,3]{1,0:T(2,128)} %copy-done.42, f32[3,272,768]{2,1,0:T(8,128)} %pad_maximum_fusion.h_ref, bf16[3,272,768]{2,1,0:T(8,128)(2,1)} %copy-done.5, bf16[3,272,768]{2,1,0:T(8,128)(2,1)} %copy-done.17, f32[3,768]{1,0:T(4,128)} %bias_ref.1), custom_call_target="tpu_custom_call" | custom-call | flops 5013504 | bytes 6266880 | tf_op jit(solution)/shard_map/finish_output/pallas_call | solution.py:519
  (350 shorter events, 186.1 us)
Async XLA Ops:
  34.3 52.1 %collective-permute-start.23 = (bf16[3,272,768]{2,1,0:T(8,128)(2,1)S(1)}, bf16[3,272,768]{2,1,0:T(8,128)(2,1)}, u32[]{:S(2)}, u32[]{:S(2)}) collective-permute-start(bf16[3,272,768]{2,1,0:T(8,128)(2,1)S(1)} %pad.8.g_ref), channel_id=1, source_target_pairs={{0,2},{2,0},{4,6},{6,4},{8,10},{10,8},{12,14},{14,12},{16,18},{18,... | collective-permute-start | bytes 3760136 | tf_op jit(solution)/shard_map/ppermute | solution.py:686
  34.4 29.0 %collective-permute-start.32 = (bf16[3,48,768]{2,1,0:T(8,128)(2,1)S(1)}, bf16[3,48,768]{2,1,0:T(8,128)(2,1)S(1)}, u32[]{:S(2)}, u32[]{:S(2)}) collective-permute-start(bf16[3,48,768]{2,1,0:T(8,128)(2,1)S(1)} %get-tuple-element.106), channel_id=1, source_target_pairs={{0,2},{2,0},{4,6},{6,4},{8,10},{10,8},{12,14},{14,12},{16,18},{18,... | collective-permute-start | bytes 663560 | tf_op jit(solution)/shard_map/ppermute | solution.py:686
  66.7 33.0 %collective-permute-start.26 = (bf16[2,3,48,768]{3,2,1,0:T(8,128)(2,1)}, bf16[2,3,48,768]{3,2,1,0:T(8,128)(2,1)}, u32[]{:S(2)}, u32[]{:S(2)}) collective-permute-start(bf16[2,3,48,768]{3,2,1,0:T(8,128)(2,1)} %pad_maximum_fusion.4.rest_0_), channel_id=1, source_target_pairs={{0,16},{2,18},{4,20},{6,22},{8,24},{10,26},{12,28},{14,30},{16,0},... | collective-permute-start | bytes 1327112 | tf_op jit(solution)/shard_map/ppermute | solution.py:686
  74.3 54.7 %collective-permute-start.28 = (bf16[2,3,48,768]{3,2,1,0:T(8,128)(2,1)}, bf16[2,3,48,768]{3,2,1,0:T(8,128)(2,1)}, u32[]{:S(2)}, u32[]{:S(2)}) collective-permute-start(bf16[2,3,48,768]{3,2,1,0:T(8,128)(2,1)} %pad_maximum_fusion.4.rest_0_), channel_id=1, source_target_pairs={{0,4},{2,6},{4,0},{6,2},{8,12},{10,14},{12,8},{14,10},{16,20},{18,... | collective-permute-start | bytes 1327112 | tf_op jit(solution)/shard_map/ppermute | solution.py:686
  75.2 32.3 %collective-permute-start.27 = (bf16[2,3,48,768]{3,2,1,0:T(8,128)(2,1)}, bf16[2,3,48,768]{3,2,1,0:T(8,128)(2,1)}, u32[]{:S(2)}, u32[]{:S(2)}) collective-permute-start(bf16[2,3,48,768]{3,2,1,0:T(8,128)(2,1)} %collective-permute-done.25.rest_1_), channel_id=1, source_target_pairs={{0,16},{2,18},{4,20},{6,22},{8,24},{10,26},{12,28},{14,30},{16,0},... | collective-permute-start | bytes 1327112 | tf_op jit(solution)/shard_map/ppermute | solution.py:686
  99.6 29.4 %collective-permute-start.29 = (bf16[2,3,48,768]{3,2,1,0:T(8,128)(2,1)}, bf16[2,3,48,768]{3,2,1,0:T(8,128)(2,1)S(1)}, u32[]{:S(2)}, u32[]{:S(2)}) collective-permute-start(bf16[2,3,48,768]{3,2,1,0:T(8,128)(2,1)} %collective-permute-done.25.rest_1_), channel_id=1, source_target_pairs={{0,4},{2,6},{4,0},{6,2},{8,12},{10,14},{12,8},{14,10},{16,20},{18,... | collective-permute-start | bytes 1327112 | tf_op jit(solution)/shard_map/ppermute | solution.py:686
  127.6 31.2 %collective-permute-start.33 = (bf16[2,3,48,768]{3,2,1,0:T(8,128)(2,1)S(1)}, bf16[2,3,48,768]{3,2,1,0:T(8,128)(2,1)}, u32[]{:S(2)}, u32[]{:S(2)}) collective-permute-start(bf16[2,3,48,768]{3,2,1,0:T(8,128)(2,1)S(1)} %pad_maximum_fusion.5.rest_0_.rest_8_), channel_id=1, source_target_pairs={{0,8},{2,10},{4,12},{6,14},{8,0},{10,2},{12,4},{14,6},{16,24},{18,... | collective-permute-start | bytes 1327112 | tf_op jit(solution)/shard_map/ppermute | solution.py:686
  151.3 45.8 %collective-permute-start.65 = (bf16[4,3,48,768]{3,2,1,0:T(8,128)(2,1)}, bf16[4,3,48,768]{3,2,1,0:T(8,128)(2,1)}, u32[]{:S(2)}, u32[]{:S(2)}) collective-permute-start(bf16[4,3,48,768]{3,2,1,0:T(8,128)(2,1)} %slice.227), channel_id=1, source_target_pairs={{0,4},{2,6},{4,0},{6,2},{8,12},{10,14},{12,8},{14,10},{16,20},{18,... | collective-permute-start | bytes 2654216 | tf_op jit(solution)/shard_map/ppermute | solution.py:686
  154.6 45.0 %collective-permute-start.62 = (bf16[4,3,48,768]{3,2,1,0:T(8,128)(2,1)}, bf16[4,3,48,768]{3,2,1,0:T(8,128)(2,1)}, u32[]{:S(2)}, u32[]{:S(2)}) collective-permute-start(bf16[4,3,48,768]{3,2,1,0:T(8,128)(2,1)} %slice.221), channel_id=1, source_target_pairs={{0,4},{2,6},{4,0},{6,2},{8,12},{10,14},{12,8},{14,10},{16,20},{18,... | collective-permute-start | bytes 2654216 | tf_op jit(solution)/shard_map/ppermute | solution.py:686
  155.5 31.1 %collective-permute-start.34 = (bf16[2,3,48,768]{3,2,1,0:T(8,128)(2,1)S(1)}, bf16[2,3,48,768]{3,2,1,0:T(8,128)(2,1)}, u32[]{:S(2)}, u32[]{:S(2)}) collective-permute-start(bf16[2,3,48,768]{3,2,1,0:T(8,128)(2,1)S(1)} %pad_maximum_fusion.5.rest_0_.rest_8_), channel_id=1, source_target_pairs={{0,16},{2,18},{4,20},{6,22},{8,24},{10,26},{12,28},{14,30},{16,0},... | collective-permute-start | bytes 1327112 | tf_op jit(solution)/shard_map/ppermute | solution.py:686
  158.8 37.1 %collective-permute-start.35 = (bf16[2,3,48,768]{3,2,1,0:T(8,128)(2,1)}, bf16[2,3,48,768]{3,2,1,0:T(8,128)(2,1)}, u32[]{:S(2)}, u32[]{:S(2)}) collective-permute-start(bf16[2,3,48,768]{3,2,1,0:T(8,128)(2,1)} %collective-permute-done.33.rest_1_.rest_9_), channel_id=1, source_target_pairs={{0,16},{2,18},{4,20},{6,22},{8,24},{10,26},{12,28},{14,30},{16,0},... | collective-permute-start | bytes 1327112 | tf_op jit(solution)/shard_map/ppermute | solution.py:686
  160.5 42.0 %collective-permute-start.36 = (bf16[2,3,48,768]{3,2,1,0:T(8,128)(2,1)S(1)}, bf16[2,3,48,768]{3,2,1,0:T(8,128)(2,1)}, u32[]{:S(2)}, u32[]{:S(2)}) collective-permute-start(bf16[2,3,48,768]{3,2,1,0:T(8,128)(2,1)S(1)} %pad_maximum_fusion.5.rest_0_.rest_8_), channel_id=1, source_target_pairs={{0,4},{2,6},{4,0},{6,2},{8,12},{10,14},{12,8},{14,10},{16,20},{18,... | collective-permute-start | bytes 1327112 | tf_op jit(solution)/shard_map/ppermute | solution.py:686
  197.1 31.8 %collective-permute-start.39 = (bf16[2,3,48,768]{3,2,1,0:T(8,128)(2,1)}, bf16[2,3,48,768]{3,2,1,0:T(8,128)(2,1)}, u32[]{:S(2)}, u32[]{:S(2)}) collective-permute-start(bf16[2,3,48,768]{3,2,1,0:T(8,128)(2,1)} %collective-permute-done.35.rest_3_.rest_11_), channel_id=1, source_target_pairs={{0,4},{2,6},{4,0},{6,2},{8,12},{10,14},{12,8},{14,10},{16,20},{18,... | collective-permute-start | bytes 1327112 | tf_op jit(solution)/shard_map/ppermute | solution.py:686
  199.6 59.5 %collective-permute-start.66 = (bf16[2,3,48,768]{3,2,1,0:T(8,128)(2,1)S(1)}, bf16[2,3,48,768]{3,2,1,0:T(8,128)(2,1)}, u32[]{:S(2)}, u32[]{:S(2)}) collective-permute-start(bf16[2,3,48,768]{3,2,1,0:T(8,128)(2,1)S(1)} %slice.264), channel_id=1, source_target_pairs={{0,16},{2,18},{4,20},{6,22},{8,24},{10,26},{12,28},{14,30},{16,0},... | collective-permute-start | bytes 1327112 | tf_op jit(solution)/shard_map/ppermute | solution.py:686
  202.6 63.1 %collective-permute-start.63 = (bf16[2,3,48,768]{3,2,1,0:T(8,128)(2,1)S(1)}, bf16[2,3,48,768]{3,2,1,0:T(8,128)(2,1)S(1)}, u32[]{:S(2)}, u32[]{:S(2)}) collective-permute-start(bf16[2,3,48,768]{3,2,1,0:T(8,128)(2,1)S(1)} %slice.260), channel_id=1, source_target_pairs={{0,16},{2,18},{4,20},{6,22},{8,24},{10,26},{12,28},{14,30},{16,0},... | collective-permute-start | bytes 1327112 | tf_op jit(solution)/shard_map/ppermute | solution.py:686
  259.2 111.2 %collective-permute-start.40 = (bf16[3,272,768]{2,1,0:T(8,128)(2,1)}, bf16[3,272,768]{2,1,0:T(8,128)(2,1)}, u32[]{:S(2)}, u32[]{:S(2)}) collective-permute-start(bf16[3,272,768]{2,1,0:T(8,128)(2,1)} %slice.242), channel_id=1, source_target_pairs={{0,2},{2,0},{4,6},{6,4},{8,10},{10,8},{12,14},{14,12},{16,18},{18,... | collective-permute-start | bytes 3760136 | tf_op jit(solution)/shard_map/ppermute | solution.py:686
  261.5 56.0 %collective-permute-start.67 = (bf16[1,3,48,768]{3,2,1,0:T(8,128)(2,1)}, bf16[1,3,48,768]{3,2,1,0:T(8,128)(2,1)}, u32[]{:S(2)}, u32[]{:S(2)}) collective-permute-start(bf16[1,3,48,768]{3,2,1,0:T(8,128)(2,1)} %slice.266), channel_id=1, source_target_pairs={{0,8},{2,10},{4,12},{6,14},{8,0},{10,2},{12,4},{14,6},{16,24},{18,... | collective-permute-start | bytes 663560 | tf_op jit(solution)/shard_map/ppermute | solution.py:686
  265.8 27.0 %collective-permute-start.46 = (bf16[272,768]{1,0:T(8,128)(2,1)S(1)}, bf16[272,768]{1,0:T(8,128)(2,1)}, u32[]{:S(2)}, u32[]{:S(2)}) collective-permute-start(bf16[272,768]{1,0:T(8,128)(2,1)S(1)} %get-tuple-element.96.dm_ref), channel_id=1, source_target_pairs={{0,1},{1,0},{2,3},{3,2},{4,5},{5,4},{6,7},{7,6},{8,9},{9,8},{10,11... | collective-permute-start | bytes 1253384 | tf_op jit(solution)/shard_map/ppermute | solution.py:732
  281.7 49.8 %collective-permute-start.58 = (bf16[4,3,48,768]{3,2,1,0:T(8,128)(2,1)S(1)}, bf16[4,3,48,768]{3,2,1,0:T(8,128)(2,1)}, u32[]{:S(2)}, u32[]{:S(2)}) collective-permute-start(bf16[4,3,48,768]{3,2,1,0:T(8,128)(2,1)S(1)} %slice.215), channel_id=1, source_target_pairs={{0,4},{2,6},{4,0},{6,2},{8,12},{10,14},{12,8},{14,10},{16,20},{18,... | collective-permute-start | bytes 2654216 | tf_op jit(solution)/shard_map/ppermute | solution.py:686
  292.8 46.5 %collective-permute-start.55 = (bf16[4,3,48,768]{3,2,1,0:T(8,128)(2,1)}, bf16[4,3,48,768]{3,2,1,0:T(8,128)(2,1)}, u32[]{:S(2)}, u32[]{:S(2)}) collective-permute-start(bf16[4,3,48,768]{3,2,1,0:T(8,128)(2,1)} %slice.209), channel_id=1, source_target_pairs={{0,4},{2,6},{4,0},{6,2},{8,12},{10,14},{12,8},{14,10},{16,20},{18,... | collective-permute-start | bytes 2654216 | tf_op jit(solution)/shard_map/ppermute | solution.py:686
  331.4 37.0 %collective-permute-start.51 = (bf16[8,4,48,384]{3,2,1,0:T(8,128)(2,1)}, bf16[8,4,48,384]{3,2,1,0:T(8,128)(2,1)S(1)}, u32[]{:S(2)}, u32[]{:S(2)}) collective-permute-start(bf16[8,4,48,384]{3,2,1,0:T(8,128)(2,1)} %get-tuple-element.79), channel_id=1, source_target_pairs={{0,2},{2,0},{4,6},{6,4},{8,10},{10,8},{12,14},{14,12},{16,18},{18,... | collective-permute-start | bytes 3538952 | tf_op jit(solution)/shard_map/ppermute | solution.py:686
  359.1 29.8 %collective-permute-start.64 = (bf16[1,3,48,768]{3,2,1,0:T(8,128)(2,1)}, bf16[1,3,48,768]{3,2,1,0:T(8,128)(2,1)}, u32[]{:S(2)}, u32[]{:S(2)}) collective-permute-start(bf16[1,3,48,768]{3,2,1,0:T(8,128)(2,1)} %slice.262), channel_id=1, source_target_pairs={{0,8},{2,10},{4,12},{6,14},{8,0},{10,2},{12,4},{14,6},{16,24},{18,... | collective-permute-start | bytes 663560 | tf_op jit(solution)/shard_map/ppermute | solution.py:686
  362.1 30.0 %collective-permute-start.68 = (f32[3,48,768]{2,1,0:T(8,128)S(1)}, f32[3,48,768]{2,1,0:T(8,128)}, u32[]{:S(2)}, u32[]{:S(2)}) collective-permute-start(f32[3,48,768]{2,1,0:T(8,128)S(1)} %copy-done.21), channel_id=1, source_target_pairs={{0,2},{2,0},{4,6},{6,4},{8,10},{10,8},{12,14},{14,12},{16,18},{18,... | collective-permute-start | bytes 1327112 | tf_op jit(solution)/shard_map/ppermute | solution.py:686
  382.2 29.1 %collective-permute-start.41 = (bf16[3,272,768]{2,1,0:T(8,128)(2,1)S(1)}, bf16[3,272,768]{2,1,0:T(8,128)(2,1)S(1)}, u32[]{:S(2)}, u32[]{:S(2)}) collective-permute-start(bf16[3,272,768]{2,1,0:T(8,128)(2,1)S(1)} %add_convert_fusion.zm_ref), channel_id=1, source_target_pairs={{0,1},{1,0},{2,3},{3,2},{4,5},{5,4},{6,7},{7,6},{8,9},{9,8},{10,11... | collective-permute-start | bytes 3760136 | tf_op jit(solution)/shard_map/ppermute | solution.py:732
  (102 other events, 1364.5 us)
